TPU v7x, 512 devices: a whole 4x8x8 slice. The times are simulated.
512 devices in a mesh: proto: 64 (over y, x, core), sample: 8 (over z).
Axes of the slice: x: 4, y: 8, z: 8, core: 2. Of those that a mesh axis runs over, the one named last changes fastest.
Arguments:
- teacher_new: bfloat16 [2048, 384], P('sample'), may hold values from -6 to 6
- queue: bfloat16 [6144, 384], P('sample'), may hold values from -6 to 6
- student: bfloat16 [2048, 384], P('sample'), may hold values from -6 to 6
- prototypes: bfloat16 [131072, 384], P('proto'), may hold values from -1 to 1
- owners: int32 [2048, 1], P('sample'), may hold values from 0 to 7; in each aligned block of 256 rows (0 to 255, 256 to 511, ...) at most 64 rows name the same one
- queue_oldest_slot: int32 [8], P('sample'), may hold values from 0 to 767
Outputs:
- new_queue: bfloat16 [6144, 384], P('sample')
- proto_grad: float32 [131072, 384], P(('proto', 'sample'))
- loss: float32 [], replicated
Inputs may be any that keep to these rules, and one draw needn't show every extreme that they name: `owners`: among the rows of one device (aligned blocks of 256 rows), no owner is named more than 64 times, a bound that some block reaches.
All inputs are finite; a program needn't handle non-finite values.
Results may differ from a plain program's by a relative error of at most 0.0034.
Values may be sent and summed in bfloat16 or wider, within the bound.
No kernel may reach another device: no remote copies, remote signals or barrier semaphores. Data moves between devices by JAX's collectives and lax.ppermute only.
A program may use at most 64 MiB of HBM per device.

v0:
```python
import jax
import jax.numpy as jnp
from jax import lax
from jax.sharding import Mesh
from jax.sharding import PartitionSpec as P

FEATURE_WIDTH = 384
K_DEV = 2048
NEW_DEV = 256
ITERS = 3
QUEUE_PER_INDEX = 768
PROTO = ("proto_0", "proto_1", "proto_2")
PROTO_SAMPLE = ("proto_0", "proto_1", "proto_2", "sample")


teacher_temp = 0.07
student_temp = 0.1
epsilon = 1e-12


def from_everyone(value, axis):
    copies = jnp.broadcast_to(value, (lax.axis_size(axis), *value.shape))
    return lax.all_to_all(copies, axis, split_axis=0, concat_axis=0, tiled=True)


def over_copies(value, axis):
    everything = from_everyone(value, axis)
    return jnp.sum(everything, axis=0)


def over_axes(value, axes):
    for axis in axes:
        value = lax.psum(value, axis)
    return value


def prefix(part, axis, combine, identity):
    place = lax.axis_index(axis)
    gathered = lax.all_gather(part, axis)
    state = jnp.zeros_like(part) + jnp.asarray(identity, part.dtype)

    def one(turn, state):
        return combine(state, lax.dynamic_index_in_dim(gathered, turn, 0, False))

    return lax.fori_loop(0, place, one, state)


def unit_rows(values):
    widened = values.astype(jnp.float32)
    length = jnp.sqrt(jnp.sum(widened * widened, axis=1, keepdims=True) + epsilon)
    return (widened / length, length)


def against(left, right):
    return lax.dot_general(
        left, right, (((1,), (1,)), ((), ())), preferred_element_type=jnp.float32
    )


def across_rows(left, right):
    return lax.dot_general(
        left, right, (((0,), (0,)), ((), ())), preferred_element_type=jnp.float32
    )


def on_device(teacher_new, queue, student, prototypes, owners, queue_oldest_slot):
    n_sample = lax.axis_size("sample")
    n_proto = lax.axis_size(PROTO)
    protos_total = K_DEV * n_proto
    teachers_total = (NEW_DEV + QUEUE_PER_INDEX) * n_sample
    new_total = NEW_DEV * n_sample
    my_index = lax.axis_index("sample")
    teacher_hat = unit_rows(jnp.concatenate([teacher_new, queue], 0))[0].astype(jnp.bfloat16)
    proto_unit, proto_length = unit_rows(prototypes)
    proto_hat = proto_unit.astype(jnp.bfloat16)
    student_normalized = unit_rows(student)[0].astype(jnp.bfloat16)
    logits = against(student_normalized, proto_hat) / student_temp
    exp_logits = jnp.exp(logits)
    denominator = over_copies(jnp.sum(exp_logits, axis=1), PROTO)
    exp_scores = jnp.exp(against(teacher_hat, proto_hat) / teacher_temp)
    row_scale = jnp.ones((exp_scores.shape[0],), jnp.float32)
    proto_scale = jnp.ones((K_DEV,), jnp.float32)
    for iteration in range(ITERS):
        column_sums = over_copies(
            jnp.dot(row_scale, exp_scores, precision=lax.Precision.HIGHEST), "sample"
        )
        proto_scale = 1.0 / (protos_total * column_sums)
        row_totals = over_copies(
            jnp.dot(exp_scores, proto_scale, precision=lax.Precision.HIGHEST), PROTO
        )
        row_scale = 1.0 / (teachers_total * row_totals)
    targets = (
        exp_scores[:NEW_DEV] * proto_scale[None, :] * row_scale[:NEW_DEV, None] * teachers_total
    )
    local_loss = jnp.sum(jnp.log(denominator)) / n_proto - jnp.sum(targets * logits)
    loss = over_axes(local_loss, PROTO_SAMPLE) / new_total
    softmax_output = exp_logits / denominator[:, None]
    grad_scale = protos_total * NEW_DEV // 32
    logit_gradient = (grad_scale * (softmax_output - targets) / (new_total * student_temp)).astype(
        jnp.bfloat16
    )
    share = K_DEV // n_sample
    columns = lax.all_to_all(logit_gradient, "sample", split_axis=1, concat_axis=0, tiled=True)
    all_students = lax.all_gather(student_normalized, "sample", axis=0, tiled=True)
    unit_gradient = across_rows(columns, all_students)
    my_unit = lax.dynamic_slice_in_dim(proto_unit, my_index * share, share, 0)
    my_length = lax.dynamic_slice_in_dim(proto_length, my_index * share, share, 0)
    proto_grad = (
        unit_gradient - my_unit * jnp.sum(my_unit * unit_gradient, axis=1, keepdims=True)
    ) / my_length
    my_head = queue_oldest_slot[0]
    owner_list = owners[:, 0]
    owner_range = jnp.arange(n_sample, dtype=jnp.int32)
    onehot = (owner_list[:, None] == owner_range[None, :]).astype(jnp.int32)
    counts_here = jnp.sum(onehot, axis=0)

    def combine(earlier, later):
        return earlier + later

    before = prefix(counts_here, "sample", combine, jnp.zeros_like(counts_here))
    local_rank = jnp.sum((jnp.cumsum(onehot, axis=0) - onehot) * onehot, axis=1)
    global_rank = local_rank + jnp.sum(onehot * before[None, :], axis=1)
    capacity = 2 * NEW_DEV // n_sample
    position = owner_list * capacity + local_rank
    row_buffer = (
        jnp.zeros((n_sample * capacity, FEATURE_WIDTH), jnp.bfloat16).at[position].set(teacher_new)
    )
    rank_buffer = jnp.full((n_sample * capacity,), -1, jnp.int32).at[position].set(global_rank)
    got_rows, got_rank = (
        lax.all_to_all(
            row_buffer.reshape(n_sample, capacity, FEATURE_WIDTH),
            "sample",
            split_axis=0,
            concat_axis=0,
            tiled=True,
        ),
        lax.all_to_all(
            rank_buffer.reshape(n_sample, capacity),
            "sample",
            split_axis=0,
            concat_axis=0,
            tiled=True,
        ),
    )
    flat_rank = got_rank.reshape(-1)
    slot_index = jnp.where(flat_rank >= 0, (my_head + flat_rank) % QUEUE_PER_INDEX, QUEUE_PER_INDEX)
    new_queue = queue.at[slot_index].set(got_rows.reshape(-1, FEATURE_WIDTH), mode="drop")
    return (new_queue, proto_grad, loss)


def solution(mesh):
    split = Mesh(
        mesh.devices.reshape(8, 4, 2, mesh.shape["sample"]),
        ("proto_0", "proto_1", "proto_2", "sample"),
    )
    return jax.shard_map(
        on_device,
        mesh=split,
        in_specs=(
            P("sample", None),
            P("sample", None),
            P("sample", None),
            P(PROTO, None),
            P("sample", None),
            P("sample"),
        ),
        out_specs=(P("sample", None), P(PROTO_SAMPLE, None), P()),
        check_vma=False,
    )
```

profile of v0, /device:TPU:8, one launch (start us, length us, event | category | flops | bytes accessed | tf_op | source)
XLA Modules:
  0.0 287.2 jit_solution(289603457188422727)
XLA Ops:
  7.2 1.2 copy.40
  8.4 1.8 fusion
  10.2 0.2 fusion.3
  10.4 2.6 multiply_exponential_fusion
  13.1 4.0 %fusion.17 = f32[1,2048]{1,0:T(1,128)S(1)} fusion(f32[1024,2048]{1,0:T(8,128)S(1)} %multiply_exponential_fusion), kind=kOutput, calls=%fused_computation.55 | convolution fusion | flops 25165824 | bytes 8396800 | tf_op jit(solution)/shard_map/dot_general | solution.py:85
  17.1 18.5 %all_to_all.75 = f32[8,1,2048]{2,1,0:T(1,128)S(1)} all-to-all(f32[8,1,2048]{2,1,0:T(1,128)S(1)} %broadcast_in_dim.44), channel_id=1, replica_groups=mesh['proto_0'=8,'proto_1'=4,'proto_2'=2,'sample'=8] {'sample'}, dimensions={0} | all-to-all | bytes 131072 | tf_op jit(solution)/shard_map/all_to_all | solution.py:23
  35.7 9.4 %fusion.23 = f32[1,1024]{1,0:T(1,128)S(1)} fusion(f32[1024,2048]{1,0:T(8,128)} %copy-done, f32[2048,1]{0,1:T(1,128)S(1)} %bitcast.57), kind=kOutput, calls=%fused_computation.63 | convolution fusion | flops 25165824 | bytes 8400896 | tf_op jit(solution)/shard_map/dot_general | solution.py:89
  45.1 0.1 broadcast_in_dim.45
  45.3 22.6 %all_to_all.76 = f32[64,1,1024]{2,1,0:T(1,128)S(1)} all-to-all(f32[64,1,1024]{2,1,0:T(1,128)S(1)} %broadcast_in_dim.45), channel_id=1, replica_groups=mesh['proto_0'=8,'proto_1'=4,'proto_2'=2,'sample'=8] {'proto_0','proto_1..., dimensions={0} | all-to-all | bytes 524288 | tf_op jit(solution)/shard_map/all_to_all | solution.py:23
  67.8 0.2 reduce_sum.165
  68.0 6.4 %fusion.24 = f32[1,2048]{1,0:T(1,128)S(1)} fusion(f32[1024,1]{0,1:T(1,128)S(1)} %bitcast.62, f32[1024,2048]{1,0:T(8,128)} %copy-done), kind=kOutput, calls=%fused_computation.64 | convolution fusion | flops 25165824 | bytes 8400896 | tf_op jit(solution)/shard_map/dot_general | solution.py:85
  74.4 0.7 broadcast_in_dim.46
  75.1 3.4 %all-to-all-start.5 = ((f32[8,1,2048]{2,1,0:T(1,128)}), f32[8,1,2048]{2,1,0:T(1,128)S(1)}, u32[]{:S(2)}, u32[]{:S(2)}) async-start(f32[8,1,2048]{2,1,0:T(1,128)} %broadcast_in_dim.46), calls=%async_computation.5 | async-start | bytes 131072 | tf_op jit(solution)/shard_map/all_to_all | solution.py:23
  78.5 0.1 fusion.9
  78.6 8.4 %all-to-all-done.5 = f32[8,1,2048]{2,1,0:T(1,128)S(1)} async-done(((f32[8,1,2048]{2,1,0:T(1,128)}), f32[8,1,2048]{2,1,0:T(1,128)S(1)}, u32[]{:S(2)}, u32[]{:S(2)}) %all-to-all-start.5) | async-done | bytes 65568 | tf_op jit(solution)/shard_map/all_to_all | solution.py:23
  87.1 9.4 %fusion.25 = f32[1,1024]{1,0:T(1,128)S(1)} fusion(f32[1024,2048]{1,0:T(8,128)} %copy-done, f32[2048,1]{0,1:T(1,128)S(1)} %bitcast.58), kind=kOutput, calls=%fused_computation.65 | convolution fusion | flops 25165824 | bytes 8400896 | tf_op jit(solution)/shard_map/dot_general | solution.py:89
  96.5 0.8 broadcast_in_dim.47
  97.3 5.4 %all-to-all-start.6 = ((f32[64,1,1024]{2,1,0:T(1,128)}), f32[64,1,1024]{2,1,0:T(1,128)S(1)}, u32[]{:S(2)}, u32[]{:S(2)}) async-start(f32[64,1,1024]{2,1,0:T(1,128)} %broadcast_in_dim.47), calls=%async_computation.6 | async-start | bytes 524288 | tf_op jit(solution)/shard_map/all_to_all | solution.py:23
  102.8 0.8 fusion.10
  103.6 1.3 dynamic-slice.4
  105.5 0.1 convert_reduce_fusion
  105.6 0.2 dynamic-update-slice
  105.9 10.2 %all-reduce = s32[64]{0:T(128)S(1)} all-reduce(s32[64]{0:T(128)S(1)} %dynamic-update-slice), channel_id=2, replica_groups=mesh['proto_0'=8,'proto_1'=4,'proto_2'=2,'sample'=8] {'sample'}, use_global_device_ids=true, to_apply=%add | all-reduce | flops 64 | bytes 512
  116.1 0.1 reshape.185
  116.2 0.2 reduce_sum.167
  116.4 6.3 %fusion.26 = f32[1,2048]{1,0:T(1,128)S(1)} fusion(f32[1024,1]{0,1:T(1,128)S(1)} %bitcast.63, f32[1024,2048]{1,0:T(8,128)} %copy-done), kind=kOutput, calls=%fused_computation.66 | convolution fusion | flops 25165824 | bytes 8400896 | tf_op jit(solution)/shard_map/dot_general | solution.py:85
  122.7 0.7 broadcast_in_dim.48
  123.4 5.0 %all-to-all-start.7 = ((f32[8,1,2048]{2,1,0:T(1,128)}), f32[8,1,2048]{2,1,0:T(1,128)S(1)}, u32[]{:S(2)}, u32[]{:S(2)}) async-start(f32[8,1,2048]{2,1,0:T(1,128)} %broadcast_in_dim.48), calls=%async_computation.7 | async-start | bytes 131072 | tf_op jit(solution)/shard_map/all_to_all | solution.py:23
  128.4 0.2 while.10
  128.7 8.6 %all-to-all-done.7 = f32[8,1,2048]{2,1,0:T(1,128)S(1)} async-done(((f32[8,1,2048]{2,1,0:T(1,128)}), f32[8,1,2048]{2,1,0:T(1,128)S(1)}, u32[]{:S(2)}, u32[]{:S(2)}) %all-to-all-start.7) | async-done | bytes 65568 | tf_op jit(solution)/shard_map/all_to_all | solution.py:23
  137.4 9.5 %fusion.27 = f32[1,1024]{1,0:T(1,128)S(1)} fusion(f32[1024,2048]{1,0:T(8,128)} %copy-done, f32[2048,1]{0,1:T(1,128)S(1)} %bitcast.53), kind=kOutput, calls=%fused_computation.67 | convolution fusion | flops 25165824 | bytes 8400896 | tf_op jit(solution)/shard_map/dot_general | solution.py:89
  146.8 0.8 broadcast_in_dim.49
  147.7 10.4 %all-to-all-start.8 = ((f32[64,1,1024]{2,1,0:T(1,128)}), f32[64,1,1024]{2,1,0:T(1,128)S(1)}, u32[]{:S(2)}, u32[]{:S(2)}) async-start(f32[64,1,1024]{2,1,0:T(1,128)} %broadcast_in_dim.49), calls=%async_computation.8 | async-start | bytes 524288 | tf_op jit(solution)/shard_map/all_to_all | solution.py:23
  158.1 0.6 reduce-window.6
  158.7 0.2 slice_reduce_fusion
  159.0 0.1 select_reduce_fusion
  159.1 1.4 scatter_custom_fusion
  160.5 0.7 all_to_all.51
  161.2 9.1 %all-to-all-done.8 = f32[64,1,1024]{2,1,0:T(1,128)S(1)} async-done(((f32[64,1,1024]{2,1,0:T(1,128)}), f32[64,1,1024]{2,1,0:T(1,128)S(1)}, u32[]{:S(2)}, u32[]{:S(2)}) %all-to-all-start.8) | async-done | bytes 262176 | tf_op jit(solution)/shard_map/all_to_all | solution.py:23
  170.3 3.3 %all-to-all-start = ((s32[8,1,64]{2,1,0:T(1,128)}), s32[8,1,64]{2,1,0:T(1,128)S(1)}, u32[]{:S(2)}, u32[]{:S(2)}) async-start(s32[8,1,64]{2,1,0:T(1,128)} %all_to_all.51), calls=%async_computation | async-start | bytes 8192 | tf_op jit(solution)/shard_map/all_to_all | solution.py:137
  173.6 0.2 reduce_sum.169
  173.8 4.3 %multiply_reduce_fusion = (f32[]{:T(128)}, f32[256]{0:T(256)S(1)}, f32[256,2048]{1,0:T(8,128)}) fusion(f32[1024,2048]{1,0:T(8,128)} %copy-done, f32[256]{0:T(256)S(1)} %slice.15, f32[2048]{0:T(1024)S(1)} %multiply_divide_fusion, bf16[256,384]{1,0:T(8,128)(2,1)S(1)} %copy-done.5, f32[2048]{0:T(1024)S(1)} %add_sqrt_fusion, bf16[2048,384]{1,0:T(8,128)(2,1)S(1)} %copy-done.2), kind=kOutput, calls=%fused_computation.12 | convolution fusion | flops 408682240 | bytes 5982212 | tf_op jit(solution)/shard_map/dot_general | solution.py:55
  178.1 3.1 %all-to-all-done = s32[8,1,64]{2,1,0:T(1,128)S(1)} async-done(((s32[8,1,64]{2,1,0:T(1,128)}), s32[8,1,64]{2,1,0:T(1,128)S(1)}, u32[]{:S(2)}, u32[]{:S(2)}) %all-to-all-start) | async-done | bytes 2080 | tf_op jit(solution)/shard_map/all_to_all | solution.py:137
  181.2 0.7 broadcast_in_dim.22
  181.8 5.6 %all-to-all-start.2 = ((f32[64,1,256]{2,1,0:T(1,128)}), f32[64,1,256]{2,1,0:T(1,128)S(1)}, u32[]{:S(2)}, u32[]{:S(2)}) async-start(f32[64,1,256]{2,1,0:T(1,128)} %broadcast_in_dim.22), calls=%async_computation.2 | async-start | bytes 131072 | tf_op jit(solution)/shard_map/all_to_all | solution.py:23
  187.5 2.2 scatter_custom_fusion.1
  189.7 6.9 %all-to-all-done.2 = f32[64,1,256]{2,1,0:T(1,128)S(1)} async-done(((f32[64,1,256]{2,1,0:T(1,128)}), f32[64,1,256]{2,1,0:T(1,128)S(1)}, u32[]{:S(2)}, u32[]{:S(2)}) %all-to-all-start.2) | async-done | bytes 65568 | tf_op jit(solution)/shard_map/all_to_all | solution.py:23
  196.6 4.1 %all-to-all-start.1 = ((bf16[8,64,384]{2,1,0:T(8,128)(2,1)}), bf16[8,64,384]{2,1,0:T(8,128)(2,1)S(1)}, u32[]{:S(2)}, u32[]{:S(2)}) async-start(bf16[8,64,384]{2,1,0:T(8,128)(2,1)} %bitcast.10), calls=%async_computation.1 | async-start | bytes 786432 | tf_op jit(solution)/shard_map/all_to_all | solution.py:130
  200.7 0.1 reduce_sum.162
  200.8 2.8 multiply_convert_fusion
  203.6 1.1 copy.29
  204.7 11.0 %all-to-all-done.1 = bf16[8,64,384]{2,1,0:T(8,128)(2,1)S(1)} async-done(((bf16[8,64,384]{2,1,0:T(8,128)(2,1)}), bf16[8,64,384]{2,1,0:T(8,128)(2,1)S(1)}, u32[]{:S(2)}, u32[]{:S(2)}) %all-to-all-start.1) | async-done | bytes 393248 | tf_op jit(solution)/shard_map/all_to_all | solution.py:130
  215.7 0.7 copy-done.3
  216.4 3.6 %all-to-all-start.9 = ((bf16[256,8,256]{2,0,1:T(8,128)(2,1)}), bf16[256,8,256]{2,0,1:T(8,128)(2,1)S(1)}, u32[]{:S(2)}, u32[]{:S(2)}) async-start(bf16[256,8,256]{2,0,1:T(8,128)(2,1)} %bitcast.46), calls=%async_computation.9 | async-start | bytes 2097152 | tf_op jit(solution)/shard_map/all_to_all | solution.py:103
  220.7 2.0 convert_divide_fusion
  222.8 0.6 log_reduce_fusion
  224.7 16.0 %psum.28 = f32[]{:T(128)} all-reduce(f32[]{:T(128)S(6)} %sub.15), channel_id=1, replica_groups=mesh['proto_0'=8,'proto_1'=4,'proto_2'=2,'sample'=8] {'proto_0'}, use_global_device_ids=true, to_apply=%region_24.25 | all-reduce | flops 1 | bytes 8 | tf_op jit(solution)/shard_map/psum | solution.py:33
  240.7 0.1 ge.14
  240.8 9.1 %psum.29 = f32[]{:T(128)} all-reduce(f32[]{:T(128)} %psum.28), channel_id=1, replica_groups=mesh['proto_0'=8,'proto_1'=4,'proto_2'=2,'sample'=8] {'proto_1'}, use_global_device_ids=true, to_apply=%region_25.26 | all-reduce | flops 1 | bytes 8 | tf_op jit(solution)/shard_map/psum | solution.py:33
  249.9 3.1 %psum.30 = f32[]{:T(128)} all-reduce(f32[]{:T(128)} %psum.29), channel_id=1, replica_groups=mesh['proto_0'=8,'proto_1'=4,'proto_2'=2,'sample'=8] {'proto_2'}, use_global_device_ids=true, to_apply=%region_26.27 | all-reduce | flops 1 | bytes 8 | tf_op jit(solution)/shard_map/psum | solution.py:33
  253.0 3.4 %scatter_fusion = bf16[768,384]{1,0:T(8,128)(2,1)S(1)} fusion(bf16[768,384]{1,0:T(8,128)(2,1)S(1)} %copy.40, s32[512]{0:T(512)S(1)} %bitcast.68, bf16[512,384]{1,0:T(8,128)(2,1)} %bitcast.52), kind=kCustom, calls=%fused_computation.2 | custom fusion | bytes 1181696 | tf_op jit(solution)/shard_map/scatter | solution.py:147
  256.4 17.9 %psum.31 = f32[]{:T(128)} all-reduce(f32[]{:T(128)} %psum.30), channel_id=1, replica_groups=mesh['proto_0'=8,'proto_1'=4,'proto_2'=2,'sample'=8] {'sample'}, use_global_device_ids=true, to_apply=%region_27.28 | all-reduce | flops 1 | bytes 8 | tf_op jit(solution)/shard_map/psum | solution.py:33
  275.1 2.3 multiply_reduce_fusion.1
  277.4 1.9 subtract_divide_fusion
  (46 shorter events, 0.7 us)
Async XLA Ops:
  7.2 3.0 %copy-start.6 = (bf16[256,384]{1,0:T(8,128)(2,1)S(1)}, bf16[256,384]{1,0:T(8,128)(2,1)}, u32[]{:S(2)}) copy-start(bf16[256,384]{1,0:T(8,128)(2,1)} %param.8) | copy-start | bytes 589828
  7.2 3.3 %copy-start.2 = (bf16[2048,384]{1,0:T(8,128)(2,1)S(1)}, bf16[2048,384]{1,0:T(8,128)(2,1)}, u32[]{:S(2)}) copy-start(bf16[2048,384]{1,0:T(8,128)(2,1)} %param.11) | copy-start | bytes 4718596
  13.0 4.0 %copy-start = (f32[1024,2048]{1,0:T(8,128)}, f32[1024,2048]{1,0:T(8,128)S(1)}, u32[]{:S(2)}) copy-start(f32[1024,2048]{1,0:T(8,128)S(1)} %multiply_exponential_fusion) | copy-start | bytes 25165828
  68.0 10.4 %copy-start.4 = (bf16[256,384]{1,0:T(8,128)(2,1)S(1)}, bf16[256,384]{1,0:T(8,128)(2,1)}, u32[]{:S(2)}) copy-start(bf16[256,384]{1,0:T(8,128)(2,1)} %param.10) | copy-start | bytes 589828
  75.1 11.9 %all-to-all-start.5 = ((f32[8,1,2048]{2,1,0:T(1,128)}), f32[8,1,2048]{2,1,0:T(1,128)S(1)}, u32[]{:S(2)}, u32[]{:S(2)}) async-start(f32[8,1,2048]{2,1,0:T(1,128)} %broadcast_in_dim.46), calls=%async_computation.5 | async-start | bytes 131072 | tf_op jit(solution)/shard_map/all_to_all | solution.py:23
  87.1 18.4 %copy-start.7 = (s32[256,1]{0,1:T(1,128)S(1)}, s32[256,1]{0,1:T(1,128)}, u32[]{:S(2)}) copy-start(s32[256,1]{0,1:T(1,128)} %param.12) | copy-start | bytes 3076
  97.3 18.8 %all-to-all-start.6 = ((f32[64,1,1024]{2,1,0:T(1,128)}), f32[64,1,1024]{2,1,0:T(1,128)S(1)}, u32[]{:S(2)}, u32[]{:S(2)}) async-start(f32[64,1,1024]{2,1,0:T(1,128)} %broadcast_in_dim.47), calls=%async_computation.6 | async-start | bytes 524288 | tf_op jit(solution)/shard_map/all_to_all | solution.py:23
  102.7 172.3 %all-gather.3.cloned.1.call-start = ((), (), s32[]{:S(2)}) async-start(), calls=%async_computation.10 | async-start | bytes 1769472 | tf_op jit(solution)/shard_map/all_gather | solution.py:104
  123.4 13.9 %all-to-all-start.7 = ((f32[8,1,2048]{2,1,0:T(1,128)}), f32[8,1,2048]{2,1,0:T(1,128)S(1)}, u32[]{:S(2)}, u32[]{:S(2)}) async-start(f32[8,1,2048]{2,1,0:T(1,128)} %broadcast_in_dim.48), calls=%async_computation.7 | async-start | bytes 131072 | tf_op jit(solution)/shard_map/all_to_all | solution.py:23
  137.3 36.5 %copy-start.5 = (bf16[256,384]{1,0:T(8,128)(2,1)S(1)}, bf16[256,384]{1,0:T(8,128)(2,1)}, u32[]{:S(2)}) copy-start(bf16[256,384]{1,0:T(8,128)(2,1)} %fusion.10) | copy-start | bytes 589828
  147.7 22.6 %all-to-all-start.8 = ((f32[64,1,1024]{2,1,0:T(1,128)}), f32[64,1,1024]{2,1,0:T(1,128)S(1)}, u32[]{:S(2)}, u32[]{:S(2)}) async-start(f32[64,1,1024]{2,1,0:T(1,128)} %broadcast_in_dim.49), calls=%async_computation.8 | async-start | bytes 524288 | tf_op jit(solution)/shard_map/all_to_all | solution.py:23
  170.3 10.9 %all-to-all-start = ((s32[8,1,64]{2,1,0:T(1,128)}), s32[8,1,64]{2,1,0:T(1,128)S(1)}, u32[]{:S(2)}, u32[]{:S(2)}) async-start(s32[8,1,64]{2,1,0:T(1,128)} %all_to_all.51), calls=%async_computation | async-start | bytes 8192 | tf_op jit(solution)/shard_map/all_to_all | solution.py:137
  181.8 14.8 %all-to-all-start.2 = ((f32[64,1,256]{2,1,0:T(1,128)}), f32[64,1,256]{2,1,0:T(1,128)S(1)}, u32[]{:S(2)}, u32[]{:S(2)}) async-start(f32[64,1,256]{2,1,0:T(1,128)} %broadcast_in_dim.22), calls=%async_computation.2 | async-start | bytes 131072 | tf_op jit(solution)/shard_map/all_to_all | solution.py:23
  196.6 19.0 %all-to-all-start.1 = ((bf16[8,64,384]{2,1,0:T(8,128)(2,1)}), bf16[8,64,384]{2,1,0:T(8,128)(2,1)S(1)}, u32[]{:S(2)}, u32[]{:S(2)}) async-start(bf16[8,64,384]{2,1,0:T(8,128)(2,1)} %bitcast.10), calls=%async_computation.1 | async-start | bytes 786432 | tf_op jit(solution)/shard_map/all_to_all | solution.py:130
  215.7 0.7 copy-start.3
  216.4 58.7 %all-to-all-start.9 = ((bf16[256,8,256]{2,0,1:T(8,128)(2,1)}), bf16[256,8,256]{2,0,1:T(8,128)(2,1)S(1)}, u32[]{:S(2)}, u32[]{:S(2)}) async-start(bf16[256,8,256]{2,0,1:T(8,128)(2,1)} %bitcast.46), calls=%async_computation.9 | async-start | bytes 2097152 | tf_op jit(solution)/shard_map/all_to_all | solution.py:103
  256.4 22.8 %copy-start.1 = (bf16[768,384]{1,0:T(8,128)(2,1)}, bf16[768,384]{1,0:T(8,128)(2,1)S(1)}, u32[]{:S(2)}) copy-start(bf16[768,384]{1,0:T(8,128)(2,1)S(1)} %scatter_fusion) | copy-start | bytes 1769476
Sparse Core Ops, SparseCore 0:
  105.6 39.0 all-gather.2
where the time goes:
time: 288 us; the launch traced here: 287 us
  blocking collectives  97.4 us (34%)
  matrix products  54.2 us (19%)
  waiting for transfers between devices  47.2 us (16%)
  starting transfers between devices  40.8 us (14%)
  between operations  18.7 us (6%)
  local copies, waits for them, and re-layouts  16.6 us (6%)
  other arithmetic  12.1 us (4%)
    psum x4, blocking collectives, over_axes(): value = lax.psum(value, axis)  46.2 us
    all_to_all x2, blocking collectives, from_everyone(): return lax.all_to_all(copies, axis, split_axis=0, concat_axis=0, tiled=True)  41.1 us
    all_to_all x5, waiting for transfers between devices, from_everyone(): return lax.all_to_all(copies, axis, split_axis=0, concat_axis=0, tiled=True)  33.1 us
    all_to_all x5, starting transfers between devices, from_everyone(): return lax.all_to_all(copies, axis, split_axis=0, concat_axis=0, tiled=True)  29.8 us
    dot_general x3, matrix products, on_device(): jnp.dot(exp_scores, proto_scale, precision=lax.Precision.HIGHEST)  28.3 us
    dot_general x3, matrix products, on_device(): jnp.dot(row_scale, exp_scores, precision=lax.Precision.HIGHEST)  16.8 us
    all_to_all x1, waiting for transfers between devices, on_device(): lax.all_to_all(row_buffer.reshape(n_sample, capacity, FEATURE_WIDTH), 'sa...  11 us
    unnamed x1, blocking collectives  10.2 us
  transfers between devices with their start and end apart: 9, of which 6 were waited for; matrix products, arithmetic and copies ran while one was open for 14% of the time, Pallas kernels for 0%

commit v1 on v0

v1 whole, which is shorter than its diff:
```python
import functools
import math

import jax
import jax.numpy as jnp
from jax import lax
from jax.experimental import pallas as pl
from jax.experimental.pallas import tpu as pltpu
from jax.sharding import Mesh
from jax.sharding import PartitionSpec as P


FEATURE_WIDTH = 384
K_DEV = 2048
NEW_DEV = 256
ITERS = 3
QUEUE_PER_INDEX = 768
PROTO = ("proto_0", "proto_1", "proto_2")
PROTO_SAMPLE = ("proto_0", "proto_1", "proto_2", "sample")
ROWS = NEW_DEV + QUEUE_PER_INDEX

teacher_temp = 0.07
student_temp = 0.1
epsilon = 1e-12
TEACHER_EXP2 = math.log2(math.e) / teacher_temp
STUDENT_EXP2 = math.log2(math.e) / student_temp
F32 = jnp.float32
BF16 = jnp.bfloat16
VMEM = pl.BlockSpec(memory_space=pltpu.VMEM)
SMEM = pl.BlockSpec(memory_space=pltpu.SMEM)
MIB = 1024 * 1024


def call(body, out_shape, args, limit, flops, scratch=(), in_specs=None):
    return pl.pallas_call(
        body,
        out_shape=out_shape,
        in_specs=in_specs or [VMEM] * len(args),
        out_specs=jax.tree.map(lambda _: VMEM, out_shape),
        scratch_shapes=list(scratch),
        compiler_params=pltpu.CompilerParams(vmem_limit_bytes=limit * MIB),
        cost_estimate=pl.CostEstimate(flops=flops, bytes_accessed=0, transcendentals=0),
    )(*args)


def shape(dims, dtype=F32):
    return jax.ShapeDtypeStruct(dims, dtype)


def unit_rows(values):
    widened = values.astype(F32)
    length = jnp.sqrt(jnp.sum(widened * widened, axis=1, keepdims=True) + epsilon)
    return widened * (1.0 / length), length


def against(left, right):
    return lax.dot_general(left, right, (((1,), (1,)), ((), ())), preferred_element_type=F32)


def lane_sums(block):
    return jnp.sum(block.T, axis=0, keepdims=True)


def along_rows(row):
    return jnp.broadcast_to(row, (128, 128)).T


def scores_body(
    place_ref, new_ref, queue_ref, student_ref, proto_ref, scores_ref, cross_ref, sums_ref, partial_ref, hat, total
):
    hat[:NEW_DEV] = unit_rows(new_ref[...])[0].astype(BF16)
    hat[NEW_DEV:ROWS] = unit_rows(queue_ref[...])[0].astype(BF16)
    hat[ROWS:] = unit_rows(student_ref[...])[0].astype(BF16)
    total[...] = jnp.zeros_like(total)

    def tile(turn, carry):
        start = pl.multiple_of(turn * 256, 256)
        rows = pl.ds(start, 256)
        proto = unit_rows(proto_ref[rows, :])[0].astype(BF16)
        column = jnp.zeros((8, 256), F32)
        for part in range(ROWS // 256):
            span = slice(part * 256, part * 256 + 256)
            scores = jnp.exp2(against(hat[span], proto) * TEACHER_EXP2)
            scores_ref[span, rows] = scores
            column += jnp.sum(scores.reshape(32, 8, 256), axis=0)
        sums_ref[:, rows] = jnp.sum(column, axis=0, keepdims=True)
        product = against(hat[ROWS:], proto)
        cross_ref[:, rows] = scores_ref[:NEW_DEV, rows] * (product * (1.0 / student_temp))
        exped = jnp.exp2(product * STUDENT_EXP2)
        total[...] += exped[:, :128] + exped[:, 128:]
        return carry

    lax.fori_loop(0, K_DEV // 256, tile, 0)
    for part in range(NEW_DEV // 128):
        span = slice(part * 128, part * 128 + 128)
        partial_ref[:, span] = lane_sums(total[span])


def weigh_columns(source_ref, row, out_ref, span, block):
    def chunk(turn):
        lanes = slice(turn * 128, turn * 128 + 128)
        return source_ref[block, lanes] * row[:, lanes]

    total = chunk(0)
    for turn in range(1, K_DEV // 128):
        total += chunk(turn)
    out_ref[:, span] = lane_sums(total)


def row_totals_body(scores_ref, weight_ref, out_ref):
    row = weight_ref[...]

    def block(turn, carry):
        start = pl.multiple_of(turn * 128, 128)
        weigh_columns(scores_ref, row, out_ref, pl.ds(start, 128), pl.ds(start, 128))
        return carry

    lax.fori_loop(0, ROWS // 128, block, 0)


def last_totals_body(scores_ref, cross_ref, weight_ref, out_ref):
    row = weight_ref[...]
    for part in range(NEW_DEV // 128):
        block = slice(part * 128, part * 128 + 128)
        weigh_columns(scores_ref, row, out_ref, block, block)
        span = slice(NEW_DEV + part * 128, NEW_DEV + part * 128 + 128)
        weigh_columns(cross_ref, row, out_ref, span, block)


def column_sums_body(scores_ref, weight_ref, out_ref, total):
    total[...] = jnp.zeros_like(total)

    def block(turn, carry):
        start = pl.multiple_of(turn * 128, 128)
        weights = along_rows(weight_ref[:, pl.ds(start, 128)])
        for chunk in range(K_DEV // 128):
            lanes = slice(chunk * 128, chunk * 128 + 128)
            part = scores_ref[pl.ds(start, 128), lanes] * weights
            total[:, lanes] += jnp.sum(part.reshape(16, 8, 128), axis=0)
        return carry

    lax.fori_loop(0, ROWS // 128, block, 0)
    out_ref[...] = jnp.sum(total[...], axis=0, keepdims=True)


def gathered_body(
    factor, place_ref, owner_ref, denominator_ref, rows_ref, queue_ref, proto_ref, column_ref,
    scores_ref, soft_ref, student_ref, unit_ref, length_ref, out_ref, chosen,
):
    n_new = rows_ref.shape[0]
    share = unit_ref.shape[0]
    first = pl.multiple_of(place_ref[0] * share, share)
    unit, length = unit_rows(proto_ref[pl.ds(first, share), :])
    unit_ref[...] = unit
    length_ref[...] = length
    proto = unit.astype(BF16)
    columns = [
        along_rows(column_ref[:, pl.ds(pl.multiple_of(first + part * 128, 128), 128)] * factor)
        for part in range(share // 128)
    ]

    def tile(turn, carry):
        start = pl.multiple_of(turn * 256, 256)
        rows = pl.ds(start, 256)
        student = unit_rows(rows_ref[rows, :FEATURE_WIDTH])[0].astype(BF16)
        student_ref[rows, :] = student
        exped = jnp.exp2(against(proto, student) * STUDENT_EXP2)
        soft_ref[:, rows] = exped * (factor / denominator_ref[:, rows])
        teacher = unit_rows(rows_ref[rows, FEATURE_WIDTH:])[0].astype(BF16)
        scores = jnp.exp2(against(proto, teacher) * TEACHER_EXP2)
        for part in range(2):
            block = slice(part * 128, part * 128 + 128)
            for side in range(2):
                lanes = pl.ds(pl.multiple_of(start + side * 128, 128), 128)
                piece = scores[block, side * 128 : side * 128 + 128]
                scores_ref[block, lanes] = piece * columns[part]
        return carry

    lax.fori_loop(0, n_new // 256, tile, 0)

    mine = place_ref[0].astype(F32)
    head = place_ref[1].astype(F32)
    size = float(QUEUE_PER_INDEX)
    earlier = lax.broadcasted_iota(jnp.int32, (128, 128), 0)
    later = lax.broadcasted_iota(jnp.int32, (128, 128), 1)
    before = jnp.where(earlier < later, 1.0, 0.0).astype(BF16)
    slots = lax.broadcasted_iota(jnp.int32, (QUEUE_PER_INDEX, 128), 0).astype(F32)
    base = jnp.zeros((1, 1), F32)
    for chunk in range(n_new // 128):
        lanes = slice(chunk * 128, chunk * 128 + 128)
        named = jnp.where(owner_ref[:, lanes] == mine, 1.0, 0.0)
        ahead = jnp.dot(
            jnp.broadcast_to(named, (16, 128)).astype(BF16), before, preferred_element_type=F32
        )[:1]
        slot = head + base + ahead
        slot = jnp.where(slot >= size, slot - size, slot)
        slot = jnp.where(named > 0.5, slot, -1.0)
        chosen[:, lanes] = jnp.where(slots == slot, 1.0, 0.0).astype(BF16)
        base += jnp.sum(named, axis=1, keepdims=True)
    got = jnp.dot(chosen[...], rows_ref[:, FEATURE_WIDTH:], preferred_element_type=F32)
    turn = lax.broadcasted_iota(jnp.int32, (QUEUE_PER_INDEX, FEATURE_WIDTH), 0).astype(F32) - head
    turn = jnp.where(turn < 0.0, turn + size, turn)
    out_ref[...] = jnp.where(turn < base, got, queue_ref[...].astype(F32)).astype(BF16)


def gradient_body(
    soft_ref, scores_ref, row_ref, student_ref, unit_ref, length_ref, out_ref, gradient
):
    n_new = soft_ref.shape[1]
    for chunk in range(n_new // 128):
        lanes = slice(chunk * 128, chunk * 128 + 128)
        target = scores_ref[:, lanes] * row_ref[:, lanes]
        gradient[:, lanes] = (soft_ref[:, lanes] - target).astype(BF16)
    unit_gradient = jnp.dot(gradient[...], student_ref[...], preferred_element_type=F32)
    unit = unit_ref[...]
    along = jnp.sum(unit * unit_gradient, axis=1, keepdims=True)
    out_ref[...] = (unit_gradient - unit * along) / length_ref[...]


def from_everyone(row, axis):
    copies = jnp.broadcast_to(row[None], (lax.axis_size(axis), *row.shape))
    return lax.all_to_all(copies, axis, split_axis=0, concat_axis=0, tiled=True)


def on_device(teacher_new, queue, student, prototypes, owners, queue_oldest_slot):
    n_sample = lax.axis_size("sample")
    n_proto = lax.axis_size(PROTO)
    protos_total = K_DEV * n_proto
    teachers_total = ROWS * n_sample
    new_total = NEW_DEV * n_sample
    share = K_DEV // n_sample
    my_index = lax.axis_index("sample")
    grad_scale = protos_total * NEW_DEV // 32

    place = jnp.stack([my_index.astype(jnp.int32), queue_oldest_slot[0].astype(jnp.int32)])

    everyone = lax.all_gather(
        jnp.concatenate([student, teacher_new], axis=1), "sample", axis=0, tiled=True
    )

    scores, cross, sums, partial = call(
        scores_body,
        (shape((ROWS, K_DEV)), shape((NEW_DEV, K_DEV)), shape((1, K_DEV)), shape((1, NEW_DEV))),
        (place, teacher_new, queue, student, prototypes),
        8,
        2 * (ROWS + NEW_DEV) * K_DEV * FEATURE_WIDTH,
        [pltpu.VMEM((ROWS + NEW_DEV, FEATURE_WIDTH), BF16), pltpu.VMEM((NEW_DEV, 128), F32)],
        in_specs=[SMEM] + [VMEM] * 4,
    )
    owner_row = owners.reshape(1, NEW_DEV).astype(F32)
    got = from_everyone(jnp.concatenate([sums, owner_row], axis=1), "sample")
    all_owners = got[:, 0, K_DEV:].reshape(1, new_total)
    proto_scale = 1.0 / jnp.sum(got[:, :, :K_DEV] * protos_total, axis=0)

    denominator = None
    all_denominators = None
    for iteration in range(ITERS - 1):
        totals = call(row_totals_body, shape((1, ROWS)), (scores, proto_scale), 4, 2 * ROWS * K_DEV)
        if iteration == 0:
            totals = jnp.concatenate([totals, partial], axis=1)
        got = from_everyone(totals, PROTO)
        if iteration == 0:
            denominator = jnp.sum(got[:, :, ROWS:], axis=0)
        row_scale = 1.0 / jnp.sum(got[:, :, :ROWS] * teachers_total, axis=0)
        sums = call(
            column_sums_body,
            shape((1, K_DEV)),
            (scores, row_scale),
            4,
            2 * ROWS * K_DEV,
            [pltpu.VMEM((8, K_DEV), F32)],
        )
        if iteration == 0:
            sums = jnp.concatenate([sums, denominator], axis=1)
        got = from_everyone(sums, "sample")
        if iteration == 0:
            all_denominators = got[:, 0, K_DEV:].reshape(1, new_total)
        proto_scale = 1.0 / jnp.sum(got[:, :, :K_DEV] * protos_total, axis=0)

    totals = call(
        last_totals_body,
        shape((1, 2 * NEW_DEV)),
        (scores, cross, proto_scale),
        4,
        4 * NEW_DEV * K_DEV,
    )
    got = from_everyone(totals, PROTO)
    row_scale = 1.0 / jnp.sum(got[:, :, :NEW_DEV], axis=0)
    cross_totals = jnp.sum(got[:, :, NEW_DEV:], axis=0)
    my_loss = jnp.sum(jnp.log(denominator) - row_scale * cross_totals, axis=1, keepdims=True)
    got = from_everyone(
        jnp.concatenate([row_scale, jnp.broadcast_to(my_loss, (1, 128))], axis=1), "sample"
    )
    all_rows = got[:, 0, :NEW_DEV].reshape(1, new_total)
    loss = jnp.sum(got[:, 0, NEW_DEV]) / new_total

    all_scores, all_soft, all_students, my_unit, my_length, new_queue = call(
        functools.partial(gathered_body, grad_scale / (new_total * student_temp)),
        (
            shape((share, new_total)),
            shape((share, new_total)),
            shape((new_total, FEATURE_WIDTH), BF16),
            shape((share, FEATURE_WIDTH)),
            shape((share, 1)),
            shape((QUEUE_PER_INDEX, FEATURE_WIDTH), BF16),
        ),
        (place, all_owners, all_denominators, everyone, queue, prototypes, proto_scale),
        12,
        4 * share * new_total * FEATURE_WIDTH,
        [pltpu.VMEM((QUEUE_PER_INDEX, new_total), BF16)],
        in_specs=[SMEM] + [VMEM] * 6,
    )
    proto_grad = call(
        gradient_body,
        shape((share, FEATURE_WIDTH)),
        (all_soft, all_scores, all_rows, all_students, my_unit, my_length),
        8,
        2 * share * new_total * FEATURE_WIDTH,
        [pltpu.VMEM((share, new_total), BF16)],
    )
    return (new_queue, proto_grad, loss)


def solution(mesh):
    split = Mesh(
        mesh.devices.reshape(8, 4, 2, mesh.shape["sample"]),
        ("proto_0", "proto_1", "proto_2", "sample"),
    )
    return jax.shard_map(
        on_device,
        mesh=split,
        in_specs=(
            P("sample", None),
            P("sample", None),
            P("sample", None),
            P(PROTO, None),
            P("sample", None),
            P("sample"),
        ),
        out_specs=(P("sample", None), P(PROTO_SAMPLE, None), P()),
        check_vma=False,
    )
```

time: 288 us -> 160 us (0.56)
  the two profiles are of different devices: /device:TPU:8 before, /device:TPU:1 now
where the time goes in v1:
time: 160 us
  blocking collectives  100 us (62%)
  Pallas kernels  20.7 us (13%)
  between operations  16.7 us (10%)
  local copies, waits for them, and re-layouts  8.02 us (5%)
  waiting for transfers between devices  6.58 us (4%)
  other arithmetic  3.73 us (2%)
  starting transfers between devices  3.37 us (2%)
    all_to_all x6, blocking collectives, from_everyone(): return lax.all_to_all(copies, axis, split_axis=0, concat_axis=0, tiled=True)  100 us
    pallas_call x8, Pallas kernels, call(): pl.pallas_call(body, out_shape=out_shape, in_specs=in_specs or [VMEM] * l...  20.7 us
    all_to_all x1, waiting for transfers between devices, from_everyone(): return lax.all_to_all(copies, axis, split_axis=0, concat_axis=0, tiled=True)  6.55 us
    unnamed x16, local copies, waits for them, and re-layouts  6.22 us
    all_to_all x1, starting transfers between devices, from_everyone(): return lax.all_to_all(copies, axis, split_axis=0, concat_axis=0, tiled=True)  3.34 us
  transfers between devices with their start and end apart: 2, of which 1 were waited for; matrix products, arithmetic and copies ran while one was open for 2% of the time, Pallas kernels for 7%

profile of v1, /device:TPU:1, one launch (start us, length us, event | category | flops | bytes accessed | tf_op | source)
XLA Modules:
  0.0 159.5 jit_solution(12903159849156612119)
XLA Ops:
  7.2 0.0 all-gather.2.cloned.1.call-start
  7.2 1.8 %pad_maximum_fusion = bf16[256,768]{1,0:T(8,128)(2,1)} fusion(bf16[256,384]{1,0:T(8,128)(2,1)} %new_ref.1, bf16[256,384]{1,0:T(8,128)(2,1)} %student_ref.1), kind=kLoop, calls=%fused_computation | loop fusion | flops 786432 | bytes 786432 | tf_op jit(solution)/shard_map/concatenate | solution.py:238
  9.0 0.0 all-gather.2.cloned.1.call-update
  9.7 0.1 pad_add_fusion.place_ref
  9.8 0.0 copy-start.1
  9.8 1.4 copy-done.1
  11.2 0.0 copy-start.3
  11.2 1.1 copy-done.3
  12.2 0.0 copy-start.5
  12.2 0.9 copy-done.5
  13.2 0.0 copy-start.6
  13.2 0.9 copy-done.6
  14.1 0.0 copy-start.7
  14.1 6.4 %shard_map.85 = (f32[1024,2048]{1,0:T(8,128)S(1)}, f32[256,2048]{1,0:T(8,128)S(1)}, f32[1,2048]{1,0:T(1,128)S(1)}, f32[1,256]{1,0:T(1,128)S(1)}) custom-call(s32[2]{0:T(128)S(1)} %pad_add_fusion.place_ref, bf16[256,384]{1,0:T(8,128)(2,1)S(1)} %copy-done.5, bf16[768,384]{1,0:T(8,128)(2,1)S(1)} %copy-done.3, bf16[256,384]{1,0:T(8,128)(2,1)S(1)} %copy-done.6, ...), custom_call_target="tpu_custom_call" | custom-call | flops 2013265920 | tf_op jit(solution)/shard_map/pallas_call | solution.py:35
  20.5 0.0 copy-done.7
  20.6 18.6 %all_to_all.35 = f32[8,1,2304]{2,1,0:T(1,128)S(1)} all-to-all(f32[8,1,2304]{2,1,0:T(1,128)S(1)} %broadcast_in_dim.29), channel_id=1, replica_groups=mesh['proto_0'=8,'proto_1'=4,'proto_2'=2,'sample'=8] {'sample'}, dimensions={0} | all-to-all | bytes 147456 | tf_op jit(solution)/shard_map/all_to_all | solution.py:222
  39.2 0.1 fusion.2
  39.3 1.2 shard_map.86
  40.6 0.2 broadcast_in_dim.31
  40.8 26.5 %all_to_all.36 = f32[64,1,1280]{2,1,0:T(1,128)S(1)} all-to-all(f32[64,1,1280]{2,1,0:T(1,128)S(1)} %broadcast_in_dim.31), channel_id=1, replica_groups=mesh['proto_0'=8,'proto_1'=4,'proto_2'=2,'sample'=8] {'proto_0','proto_1..., dimensions={0} | all-to-all | bytes 655360 | tf_op jit(solution)/shard_map/all_to_all | solution.py:222
  67.3 0.1 fusion
  67.4 1.1 shard_map.87
  68.5 0.1 slice_reduce_fusion.2
  68.7 9.8 %all_to_all.37 = f32[8,1,2304]{2,1,0:T(1,128)S(1)} all-to-all(f32[8,1,2304]{2,1,0:T(1,128)S(1)} %broadcast_in_dim.65), channel_id=1, replica_groups=mesh['proto_0'=8,'proto_1'=4,'proto_2'=2,'sample'=8] {'sample'}, dimensions={0} | all-to-all | bytes 147456 | tf_op jit(solution)/shard_map/all_to_all | solution.py:222
  78.4 0.1 fusion.3
  78.5 1.2 shard_map.88
  79.7 0.1 broadcast_in_dim.67
  79.9 19.0 %all_to_all.38 = f32[64,1,1024]{2,1,0:T(1,128)S(1)} all-to-all(f32[64,1,1024]{2,1,0:T(1,128)S(1)} %broadcast_in_dim.67), channel_id=1, replica_groups=mesh['proto_0'=8,'proto_1'=4,'proto_2'=2,'sample'=8] {'proto_0','proto_1..., dimensions={0} | all-to-all | bytes 524288 | tf_op jit(solution)/shard_map/all_to_all | solution.py:222
  98.9 0.1 fusion.1
  98.9 1.1 shard_map.89
  100.1 9.5 %all_to_all.39 = f32[8,1,2048]{2,1,0:T(1,128)S(1)} all-to-all(f32[8,1,2048]{2,1,0:T(1,128)S(1)} %broadcast_in_dim.69), channel_id=1, replica_groups=mesh['proto_0'=8,'proto_1'=4,'proto_2'=2,'sample'=8] {'sample'}, dimensions={0} | all-to-all | bytes 131072 | tf_op jit(solution)/shard_map/all_to_all | solution.py:222
  109.6 0.1 multiply_reduce_fusion
  109.7 0.0 copy-start.2
  109.7 0.0 copy-start.4
  109.8 0.4 shard_map.91
  110.2 0.1 broadcast_in_dim.71
  110.2 17.0 %all_to_all.40 = f32[64,1,512]{2,1,0:T(1,128)S(1)} all-to-all(f32[64,1,512]{2,1,0:T(1,128)S(1)} %broadcast_in_dim.71), channel_id=1, replica_groups=mesh['proto_0'=8,'proto_1'=4,'proto_2'=2,'sample'=8] {'proto_0','proto_1..., dimensions={0} | all-to-all | bytes 262144 | tf_op jit(solution)/shard_map/all_to_all | solution.py:222
  127.3 0.1 slice_reduce_fusion
  127.4 0.6 subtract_reduce_fusion
  128.0 0.7 pad_reduce_fusion
  128.6 0.6 broadcast_in_dim.73
  129.3 3.3 %all-to-all-start.6 = ((f32[8,1,384]{2,1,0:T(1,128)}), f32[8,1,384]{2,1,0:T(1,128)S(1)}, u32[]{:S(2)}, u32[]{:S(2)}) async-start(f32[8,1,384]{2,1,0:T(1,128)} %broadcast_in_dim.73), calls=%async_computation.6 | async-start | bytes 24576 | tf_op jit(solution)/shard_map/all_to_all | solution.py:222
  132.6 6.5 %all-to-all-done.6 = f32[8,1,384]{2,1,0:T(1,128)S(1)} async-done(((f32[8,1,384]{2,1,0:T(1,128)}), f32[8,1,384]{2,1,0:T(1,128)S(1)}, u32[]{:S(2)}, u32[]{:S(2)}) %all-to-all-start.6) | async-done | bytes 12320 | tf_op jit(solution)/shard_map/all_to_all | solution.py:222
  139.2 0.6 slice_reduce_fusion.3
  140.4 0.0 all-gather.2.cloned.1.call-done.rows_ref
  140.5 0.0 copy-done.2
  140.5 0.0 copy-done.4
  140.5 0.0 copy-start
  140.5 1.9 %copy-done = bf16[2048,768]{1,0:T(8,128)(2,1)S(1)} copy-done((bf16[2048,768]{1,0:T(8,128)(2,1)S(1)}, bf16[2048,768]{1,0:T(8,128)(2,1)}, u32[]{:S(2)}) %copy-start) | copy-done | bytes 3145752
  142.4 7.6 %shard_map.90 = (f32[256,2048]{1,0:T(8,128)S(1)}, f32[256,2048]{1,0:T(8,128)S(1)}, bf16[2048,384]{1,0:T(8,128)(2,1)S(1)}, f32[256,384]{1,0:T(8,128)S(1)}, f32[25...) custom-call(s32[2]{0:T(128)S(1)} %pad_add_fusion.place_ref, f32[1,2048]{1,0:T(1,128)S(1)} %bitcast.19, f32[1,2048]{1,0:T(1,128)S(1)} %bitcast.20, ...), custom_call_target="tpu_custom_call" | custom-call | flops 805306368 | tf_op jit(solution)/shard_map/pallas_call | solution.py:35
  149.9 1.6 %shard_map.92 = f32[256,384]{1,0:T(8,128)} custom-call(f32[256,2048]{1,0:T(8,128)S(1)} %get-tuple-element.17.soft_ref, f32[256,2048]{1,0:T(8,128)S(1)} %get-tuple-element.18.scores_ref, f32[1,2048]{1,0:T(1,128)S(1)} %bitcast.21, bf16[2048,384]{1,0:T(8,128)(2,1)S(1)} %get-tuple-element.20.student_ref, f32[256,384]{1,0:T(8,128)S(1)} %get-tuple-element.21.unit_ref, ...), custom_call_target="tpu_custom_call" | custom-call | flops 402653184 | tf_op jit(solution)/shard_map/pallas_call | solution.py:35
  (16 shorter events, 0.3 us)
Async XLA Ops:
  7.2 133.3 %all-gather.2.cloned.1.call-start = ((), (), s32[]{:S(2)}) async-start(), calls=%async_computation.7 | async-start | bytes 3538944 | tf_op jit(solution)/shard_map/all_gather | solution.py:237
  9.8 1.4 copy-start.1
  11.2 1.1 copy-start.3
  12.2 0.9 copy-start.5
  13.2 0.9 copy-start.6
  14.1 6.4 %copy-start.7 = (s32[256,1]{0,1:T(1,128)S(1)}, s32[256,1]{0,1:T(1,128)}, u32[]{:S(2)}) copy-start(s32[256,1]{0,1:T(1,128)} %param.10) | copy-start | bytes 3076
  109.7 30.7 %copy-start.2 = (bf16[2048,384]{1,0:T(8,128)(2,1)S(1)}, bf16[2048,384]{1,0:T(8,128)(2,1)}, u32[]{:S(2)}) copy-start(bf16[2048,384]{1,0:T(8,128)(2,1)} %proto_ref.3) | copy-start | bytes 4718596
  109.7 30.7 %copy-start.4 = (bf16[768,384]{1,0:T(8,128)(2,1)S(1)}, bf16[768,384]{1,0:T(8,128)(2,1)}, u32[]{:S(2)}) copy-start(bf16[768,384]{1,0:T(8,128)(2,1)} %queue_ref.3) | copy-start | bytes 1769476
  129.3 9.9 %all-to-all-start.6 = ((f32[8,1,384]{2,1,0:T(1,128)}), f32[8,1,384]{2,1,0:T(1,128)S(1)}, u32[]{:S(2)}, u32[]{:S(2)}) async-start(f32[8,1,384]{2,1,0:T(1,128)} %broadcast_in_dim.73), calls=%async_computation.6 | async-start | bytes 24576 | tf_op jit(solution)/shard_map/all_to_all | solution.py:222
  140.5 1.9 %copy-start = (bf16[2048,768]{1,0:T(8,128)(2,1)S(1)}, bf16[2048,768]{1,0:T(8,128)(2,1)}, u32[]{:S(2)}) copy-start(bf16[2048,768]{1,0:T(8,128)(2,1)} %all-gather.2.cloned.1.call-done.rows_ref) | copy-start | bytes 9437188
Sparse Core Ops, SparseCore 0:
  10.6 55.2 all-gather.1

commit v2 on v1

--- a/solution.py
+++ b/solution.py
@@ -28,21 +28,27 @@
 BF16 = jnp.bfloat16
 VMEM = pl.BlockSpec(memory_space=pltpu.VMEM)
 SMEM = pl.BlockSpec(memory_space=pltpu.SMEM)
+HBM = pl.BlockSpec(memory_space=pltpu.HBM)
+DMA = pltpu.SemaphoreType.DMA
 MIB = 1024 * 1024
 
 
-def call(body, out_shape, args, limit, flops, scratch=(), in_specs=None):
+def call(body, out_shape, args, limit, flops, scratch=(), in_specs=None, out_specs=None):
     return pl.pallas_call(
         body,
         out_shape=out_shape,
         in_specs=in_specs or [VMEM] * len(args),
-        out_specs=jax.tree.map(lambda _: VMEM, out_shape),
+        out_specs=out_specs or jax.tree.map(lambda _: VMEM, out_shape),
         scratch_shapes=list(scratch),
         compiler_params=pltpu.CompilerParams(vmem_limit_bytes=limit * MIB),
         cost_estimate=pl.CostEstimate(flops=flops, bytes_accessed=0, transcendentals=0),
     )(*args)
 
 
+def in_hbm(value):
+    return pltpu.with_memory_space_constraint(value, pltpu.HBM)
+
+
 def shape(dims, dtype=F32):
     return jax.ShapeDtypeStruct(dims, dtype)
 
@@ -65,18 +71,51 @@
     return jnp.broadcast_to(row, (128, 128)).T
 
 
+def units_body(
+    place_ref, new_hbm, queue_hbm, student_hbm, hat_ref, half_hbm, raw, half, row_sems, half_sem
+):
+    copies = [
+        pltpu.make_async_copy(student_hbm, raw.at[pl.ds(ROWS, NEW_DEV)], row_sems.at[0]),
+        pltpu.make_async_copy(new_hbm, raw.at[pl.ds(0, NEW_DEV)], row_sems.at[1]),
+        pltpu.make_async_copy(queue_hbm, raw.at[pl.ds(NEW_DEV, QUEUE_PER_INDEX)], row_sems.at[2]),
+    ]
+    for copy in copies:
+        copy.start()
+
+    def rows_hat(turn, carry):
+        rows = pl.ds(pl.multiple_of(turn * 128, 128), 128)
+        hat_ref[rows, :] = unit_rows(raw[rows, :])[0].astype(BF16)
+        return carry
+
+    mine = place_ref[2] * 128
+    copies[0].wait()
+    lax.fori_loop(ROWS // 128, (ROWS + NEW_DEV) // 128, rows_hat, 0)
+    half[:128] = hat_ref[pl.ds(pl.multiple_of(ROWS + mine, 128), 128), :]
+    copies[1].wait()
+    half[128:] = raw[pl.ds(pl.multiple_of(mine, 128), 128), :]
+    half_copy = pltpu.make_async_copy(half, half_hbm, half_sem)
+    half_copy.start()
+    copies[2].wait()
+    lax.fori_loop(0, ROWS // 128, rows_hat, 0)
+    half_copy.wait()
+
+
 def scores_body(
-    place_ref, new_ref, queue_ref, student_ref, proto_ref, scores_ref, cross_ref, sums_ref, partial_ref, hat, total
+    hat, proto_hbm, scores_ref, cross_ref, sums_ref, partial_ref, raw_proto, total, proto_sems
 ):
-    hat[:NEW_DEV] = unit_rows(new_ref[...])[0].astype(BF16)
-    hat[NEW_DEV:ROWS] = unit_rows(queue_ref[...])[0].astype(BF16)
-    hat[ROWS:] = unit_rows(student_ref[...])[0].astype(BF16)
+    def proto_copy(turn):
+        rows = pl.ds(pl.multiple_of(turn * 256, 256), 256)
+        return pltpu.make_async_copy(proto_hbm.at[rows], raw_proto.at[rows], proto_sems.at[turn])
+
+    for turn in range(K_DEV // 256):
+        proto_copy(turn).start()
     total[...] = jnp.zeros_like(total)
 
     def tile(turn, carry):
         start = pl.multiple_of(turn * 256, 256)
         rows = pl.ds(start, 256)
-        proto = unit_rows(proto_ref[rows, :])[0].astype(BF16)
+        proto_copy(turn).wait()
+        proto = unit_rows(raw_proto[rows, :])[0].astype(BF16)
         column = jnp.zeros((8, 256), F32)
         for part in range(ROWS // 256):
             span = slice(part * 256, part * 256 + 256)
@@ -143,40 +182,61 @@
     out_ref[...] = jnp.sum(total[...], axis=0, keepdims=True)
 
 
+def message_lanes(chunk):
+    return chunk // 2, slice((chunk % 2) * 128, (chunk % 2) * 128 + 128)
+
+
 def gathered_body(
-    factor, place_ref, owner_ref, denominator_ref, rows_ref, queue_ref, proto_ref, column_ref,
-    scores_ref, soft_ref, student_ref, unit_ref, length_ref, out_ref, chosen,
+    factor, place_ref, first_ref, second_ref, everyone_hbm, queue_hbm, proto_hbm, column_ref,
+    scores_ref, soft_hbm, unit_ref, length_ref, out_ref,
+    rows_in, proto_in, queue_in, soft, chosen, row_sems, soft_sems, proto_sem, queue_sem,
 ):
-    n_new = rows_ref.shape[0]
+    n_blocks = everyone_hbm.shape[0]
+    n_new = n_blocks * 128
     share = unit_ref.shape[0]
     first = pl.multiple_of(place_ref[0] * share, share)
-    unit, length = unit_rows(proto_ref[pl.ds(first, share), :])
-    unit_ref[...] = unit
-    length_ref[...] = length
-    proto = unit.astype(BF16)
+    proto_copy = pltpu.make_async_copy(proto_hbm.at[pl.ds(first, share)], proto_in, proto_sem)
+    proto_copy.start()
+
+    def rows_copy(turn):
+        blocks = pl.ds(turn * 2, 2)
+        return pltpu.make_async_copy(everyone_hbm.at[blocks], rows_in.at[blocks], row_sems.at[turn])
+
+    def soft_copy(turn):
+        lanes = pl.ds(pl.multiple_of(turn * 256, 256), 256)
+        return pltpu.make_async_copy(soft.at[:, lanes], soft_hbm.at[:, lanes], soft_sems.at[turn])
+
+    for turn in range(n_blocks // 2):
+        rows_copy(turn).start()
+    queue_copy = pltpu.make_async_copy(queue_hbm, queue_in, queue_sem)
+    queue_copy.start()
     columns = [
         along_rows(column_ref[:, pl.ds(pl.multiple_of(first + part * 128, 128), 128)] * factor)
         for part in range(share // 128)
     ]
+    proto_copy.wait()
+    unit, length = unit_rows(proto_in[...])
+    unit_ref[...] = unit
+    length_ref[...] = length
+    proto = unit.astype(BF16)
 
     def tile(turn, carry):
         start = pl.multiple_of(turn * 256, 256)
-        rows = pl.ds(start, 256)
-        student = unit_rows(rows_ref[rows, :FEATURE_WIDTH])[0].astype(BF16)
-        student_ref[rows, :] = student
-        exped = jnp.exp2(against(proto, student) * STUDENT_EXP2)
-        soft_ref[:, rows] = exped * (factor / denominator_ref[:, rows])
-        teacher = unit_rows(rows_ref[rows, FEATURE_WIDTH:])[0].astype(BF16)
-        scores = jnp.exp2(against(proto, teacher) * TEACHER_EXP2)
-        for part in range(2):
-            block = slice(part * 128, part * 128 + 128)
-            for side in range(2):
-                lanes = pl.ds(pl.multiple_of(start + side * 128, 128), 128)
-                piece = scores[block, side * 128 : side * 128 + 128]
-                scores_ref[block, lanes] = piece * columns[part]
+        rows_copy(turn).wait()
+        for side in range(2):
+            lanes = pl.ds(pl.multiple_of(start + side * 128, 128), 128)
+            exped = jnp.exp2(against(proto, rows_in[turn * 2 + side, :128, :]) * STUDENT_EXP2)
+            names = slice(K_DEV + side * 128, K_DEV + side * 128 + 128)
+            soft[:, lanes] = exped * (factor / second_ref[turn, :, names])
+            teacher = unit_rows(rows_in[turn * 2 + side, 128:, :])[0].astype(BF16)
+            scores = jnp.exp2(against(proto, teacher) * TEACHER_EXP2)
+            for part in range(2):
+                block = slice(part * 128, part * 128 + 128)
+                scores_ref[block, lanes] = scores[block] * columns[part]
+        soft_copy(turn).start()
         return carry
 
-    lax.fori_loop(0, n_new // 256, tile, 0)
+    lax.fori_loop(0, n_blocks // 2, tile, 0)
 
     mine = place_ref[0].astype(F32)
     head = place_ref[1].astype(F32)
@@ -187,31 +247,58 @@
     slots = lax.broadcasted_iota(jnp.int32, (QUEUE_PER_INDEX, 128), 0).astype(F32)
     base = jnp.zeros((1, 1), F32)
     for chunk in range(n_new // 128):
-        lanes = slice(chunk * 128, chunk * 128 + 128)
-        named = jnp.where(owner_ref[:, lanes] == mine, 1.0, 0.0)
+        plane, lanes = message_lanes(chunk)
+        names = slice(K_DEV + lanes.start, K_DEV + lanes.stop)
+        named = jnp.where(first_ref[plane, :, names] == mine, 1.0, 0.0)
         ahead = jnp.dot(
             jnp.broadcast_to(named, (16, 128)).astype(BF16), before, preferred_element_type=F32
         )[:1]
         slot = head + base + ahead
         slot = jnp.where(slot >= size, slot - size, slot)
         slot = jnp.where(named > 0.5, slot, -1.0)
-        chosen[:, lanes] = jnp.where(slots == slot, 1.0, 0.0).astype(BF16)
+        chosen[:, chunk * 128 : chunk * 128 + 128] = jnp.where(slots == slot, 1.0, 0.0).astype(BF16)
         base += jnp.sum(named, axis=1, keepdims=True)
-    got = jnp.dot(chosen[...], rows_ref[:, FEATURE_WIDTH:], preferred_element_type=F32)
+    teachers = rows_in[:, 128:, :].reshape(n_new, FEATURE_WIDTH)
+    got = jnp.dot(chosen[...], teachers, preferred_element_type=F32)
     turn = lax.broadcasted_iota(jnp.int32, (QUEUE_PER_INDEX, FEATURE_WIDTH), 0).astype(F32) - head
     turn = jnp.where(turn < 0.0, turn + size, turn)
-    out_ref[...] = jnp.where(turn < base, got, queue_ref[...].astype(F32)).astype(BF16)
+    queue_copy.wait()
+    out_ref[...] = jnp.where(turn < base, got, queue_in[...].astype(F32)).astype(BF16)
+    for turn in range(n_blocks // 2):
+        soft_copy(turn).wait()
+
+
+def rows_body(got_ref, denominator_ref, out_ref):
+    totals = jnp.sum(got_ref[...], axis=0)
+    row_scale = 1.0 / totals[:, :NEW_DEV]
+    terms = jnp.log(denominator_ref[...]) - row_scale * totals[:, NEW_DEV:]
+    loss = jnp.broadcast_to(jnp.sum(terms, axis=1, keepdims=True), (1, 128))
+    message = jnp.concatenate([row_scale, loss], axis=1)
+    out_ref[...] = jnp.broadcast_to(message[None], out_ref.shape)
 
 
 def gradient_body(
-    soft_ref, scores_ref, row_ref, student_ref, unit_ref, length_ref, out_ref, gradient
+    got_ref, scores_ref, soft_hbm, everyone_hbm, unit_ref, length_ref, out_ref, loss_ref,
+    soft, student, gradient, soft_sem, student_sem,
 ):
-    n_new = soft_ref.shape[1]
-    for chunk in range(n_new // 128):
+    n_blocks = student.shape[0]
+    n_new = n_blocks * 128
+    soft_copy = pltpu.make_async_copy(soft_hbm, soft, soft_sem)
+    student_copy = pltpu.make_async_copy(
+        everyone_hbm.at[:, pl.ds(0, 128), :], student, student_sem
+    )
+    soft_copy.start()
+    student_copy.start()
+    loss_ref[...] = jnp.sum(got_ref[:, :, NEW_DEV : NEW_DEV + 1], axis=0) * (1.0 / n_new)
+    soft_copy.wait()
+    for chunk in range(n_blocks):
+        plane, names = message_lanes(chunk)
         lanes = slice(chunk * 128, chunk * 128 + 128)
-        target = scores_ref[:, lanes] * row_ref[:, lanes]
-        gradient[:, lanes] = (soft_ref[:, lanes] - target).astype(BF16)
-    unit_gradient = jnp.dot(gradient[...], student_ref[...], preferred_element_type=F32)
+        target = scores_ref[:, lanes] * got_ref[plane, :, names]
+        gradient[:, lanes] = (soft[:, lanes] - target).astype(BF16)
+    student_copy.wait()
+    students = student[...].reshape(n_new, FEATURE_WIDTH)
+    unit_gradient = jnp.dot(gradient[...], students, preferred_element_type=F32)
     unit = unit_ref[...]
     along = jnp.sum(unit * unit_gradient, axis=1, keepdims=True)
     out_ref[...] = (unit_gradient - unit * along) / length_ref[...]
@@ -231,29 +318,53 @@
     share = K_DEV // n_sample
     my_index = lax.axis_index("sample")
     grad_scale = protos_total * NEW_DEV // 32
-
-    place = jnp.stack([my_index.astype(jnp.int32), queue_oldest_slot[0].astype(jnp.int32)])
-
-    everyone = lax.all_gather(
-        jnp.concatenate([student, teacher_new], axis=1), "sample", axis=0, tiled=True
-    )
-
+    factor = grad_scale / (new_total * student_temp)
+    place = jnp.stack(
+        [
+            my_index.astype(jnp.int32),
+            queue_oldest_slot[0].astype(jnp.int32),
+            lax.axis_index("proto_2").astype(jnp.int32),
+        ]
+    )
+
+    hat, half = call(
+        units_body,
+        (
+            shape((ROWS + NEW_DEV, FEATURE_WIDTH), BF16),
+            pltpu.HBM((NEW_DEV, FEATURE_WIDTH), BF16),
+        ),
+        (place, in_hbm(teacher_new), in_hbm(queue), in_hbm(student)),
+        6,
+        8 * (ROWS + NEW_DEV) * FEATURE_WIDTH,
+        [
+            pltpu.VMEM((ROWS + NEW_DEV, FEATURE_WIDTH), BF16),
+            pltpu.VMEM((NEW_DEV, FEATURE_WIDTH), BF16),
+            DMA((3,)),
+            DMA,
+        ],
+        in_specs=[SMEM] + [HBM] * 3,
+        out_specs=(VMEM, HBM),
+    )
+    everyone = lax.all_gather(half, ("sample", "proto_2"), axis=0)
     scores, cross, sums, partial = call(
         scores_body,
         (shape((ROWS, K_DEV)), shape((NEW_DEV, K_DEV)), shape((1, K_DEV)), shape((1, NEW_DEV))),
-        (place, teacher_new, queue, student, prototypes),
+        (hat, in_hbm(prototypes)),
         8,
         2 * (ROWS + NEW_DEV) * K_DEV * FEATURE_WIDTH,
-        [pltpu.VMEM((ROWS + NEW_DEV, FEATURE_WIDTH), BF16), pltpu.VMEM((NEW_DEV, 128), F32)],
-        in_specs=[SMEM] + [VMEM] * 4,
+        [
+            pltpu.VMEM((K_DEV, FEATURE_WIDTH), BF16),
+            pltpu.VMEM((NEW_DEV, 128), F32),
+            DMA((K_DEV // 256,)),
+        ],
+        in_specs=[VMEM, HBM],
     )
     owner_row = owners.reshape(1, NEW_DEV).astype(F32)
-    got = from_everyone(jnp.concatenate([sums, owner_row], axis=1), "sample")
-    all_owners = got[:, 0, K_DEV:].reshape(1, new_total)
-    proto_scale = 1.0 / jnp.sum(got[:, :, :K_DEV] * protos_total, axis=0)
+    first = from_everyone(jnp.concatenate([sums, owner_row], axis=1), "sample")
+    proto_scale = 1.0 / jnp.sum(first[:, :, :K_DEV] * protos_total, axis=0)
 
     denominator = None
-    all_denominators = None
+    second = None
     for iteration in range(ITERS - 1):
         totals = call(row_totals_body, shape((1, ROWS)), (scores, proto_scale), 4, 2 * ROWS * K_DEV)
         if iteration == 0:
@@ -274,7 +385,7 @@
             sums = jnp.concatenate([sums, denominator], axis=1)
         got = from_everyone(sums, "sample")
         if iteration == 0:
-            all_denominators = got[:, 0, K_DEV:].reshape(1, new_total)
+            second = got
         proto_scale = 1.0 / jnp.sum(got[:, :, :K_DEV] * protos_total, axis=0)
 
     totals = call(
@@ -285,40 +396,53 @@
         4 * NEW_DEV * K_DEV,
     )
     got = from_everyone(totals, PROTO)
-    row_scale = 1.0 / jnp.sum(got[:, :, :NEW_DEV], axis=0)
-    cross_totals = jnp.sum(got[:, :, NEW_DEV:], axis=0)
-    my_loss = jnp.sum(jnp.log(denominator) - row_scale * cross_totals, axis=1, keepdims=True)
-    got = from_everyone(
-        jnp.concatenate([row_scale, jnp.broadcast_to(my_loss, (1, 128))], axis=1), "sample"
-    )
-    all_rows = got[:, 0, :NEW_DEV].reshape(1, new_total)
-    loss = jnp.sum(got[:, 0, NEW_DEV]) / new_total
-
-    all_scores, all_soft, all_students, my_unit, my_length, new_queue = call(
-        functools.partial(gathered_body, grad_scale / (new_total * student_temp)),
+    message = call(
+        rows_body, shape((n_sample, 1, NEW_DEV + 128)), (got, denominator), 4, n_proto * 2 * NEW_DEV
+    )
+    got = lax.all_to_all(message, "sample", split_axis=0, concat_axis=0, tiled=True)
+
+    all_scores, all_soft, my_unit, my_length, new_queue = call(
+        functools.partial(gathered_body, factor),
         (
             shape((share, new_total)),
-            shape((share, new_total)),
-            shape((new_total, FEATURE_WIDTH), BF16),
+            pltpu.HBM((share, new_total), F32),
             shape((share, FEATURE_WIDTH)),
             shape((share, 1)),
             shape((QUEUE_PER_INDEX, FEATURE_WIDTH), BF16),
         ),
-        (place, all_owners, all_denominators, everyone, queue, prototypes, proto_scale),
+        (place, first, second, in_hbm(everyone), in_hbm(queue), in_hbm(prototypes), proto_scale),
+        16,
+        4 * share * new_total * FEATURE_WIDTH,
+        [
+            pltpu.VMEM(everyone.shape, BF16),
+            pltpu.VMEM((share, FEATURE_WIDTH), BF16),
+            pltpu.VMEM((QUEUE_PER_INDEX, FEATURE_WIDTH), BF16),
+            pltpu.VMEM((share, new_total), F32),
+            pltpu.VMEM((QUEUE_PER_INDEX, new_total), BF16),
+            DMA((n_sample,)),
+            DMA((n_sample,)),
+            DMA,
+            DMA,
+        ],
+        in_specs=[SMEM, VMEM, VMEM, HBM, HBM, HBM, VMEM],
+        out_specs=(VMEM, HBM, VMEM, VMEM, VMEM),
+    )
+    proto_grad, loss = call(
+        gradient_body,
+        (shape((share, FEATURE_WIDTH)), shape((1, 1))),
+        (got, all_scores, in_hbm(all_soft), in_hbm(everyone), my_unit, my_length),
         12,
-        4 * share * new_total * FEATURE_WIDTH,
-        [pltpu.VMEM((QUEUE_PER_INDEX, new_total), BF16)],
-        in_specs=[SMEM] + [VMEM] * 6,
-    )
-    proto_grad = call(
-        gradient_body,
-        shape((share, FEATURE_WIDTH)),
-        (all_soft, all_scores, all_rows, all_students, my_unit, my_length),
-        8,
         2 * share * new_total * FEATURE_WIDTH,
-        [pltpu.VMEM((share, new_total), BF16)],
-    )
-    return (new_queue, proto_grad, loss)
+        [
+            pltpu.VMEM((share, new_total), F32),
+            pltpu.VMEM((new_total // 128, 128, FEATURE_WIDTH), BF16),
+            pltpu.VMEM((share, new_total), BF16),
+            DMA,
+            DMA,
+        ],
+        in_specs=[VMEM, VMEM, HBM, HBM, VMEM, VMEM],
+    )
+    return (new_queue, proto_grad, loss.reshape(()))
 
 
 def solution(mesh):

time: 160 us -> 148 us (0.925)
  Pallas kernels: 20.7 us -> 28.3 us
  local copies, waits for them, and re-layouts: 8.02 us -> 0.52 us
  waiting for transfers between devices: 6.58 us -> 0.04 us
  other arithmetic: 3.73 us -> 0.62 us
  between operations: 16.7 us -> 14.9 us
    pallas_call x8 -> x10, Pallas kernels: 20.7 us -> 28.3 us  [call(): pl.pallas_call(body, out_shape=out_shape, in_specs=in_specs or [VMEM] * l...]
    all_to_all x1, waiting for transfers between devices: 6.55 us -> 0.01 us  [on_device(): lax.all_to_all(message, 'sample', split_axis=0, concat_axis=0, tiled=True)]
    unnamed x16 -> x2, local copies, waits for them, and re-layouts: 6.22 us -> 0.01 us
    concatenate x2 -> x1, other arithmetic: 1.83 us -> 0.03 us  [on_device(): first = from_everyone(jnp.concatenate([sums, owner_row], axis=1), 'sample')]
  transfers between devices with their start and end apart: 2 -> 2, of which waited for: 1 -> 0; matrix products, arithmetic and copies ran while one was open for 2% -> 1% of each run, Pallas kernels for 7% -> 15%
where the time goes in v2:
time: 148 us; the launch traced here: 147 us
  blocking collectives  99.4 us (67%)
  Pallas kernels  28.3 us (19%)
  between operations  14.9 us (10%)
  starting transfers between devices  3.36 us (2%)
    all_to_all x6, blocking collectives, from_everyone(): return lax.all_to_all(copies, axis, split_axis=0, concat_axis=0, tiled=True)  99.4 us
    pallas_call x10, Pallas kernels, call(): pl.pallas_call(body, out_shape=out_shape, in_specs=in_specs or [VMEM] * l...  28.3 us
    all_to_all x1, starting transfers between devices, on_device(): lax.all_to_all(message, 'sample', split_axis=0, concat_axis=0, tiled=True)  3.32 us
  transfers between devices with their start and end apart: 2, of which 0 were waited for; matrix products, arithmetic and copies ran while one was open for 1% of the time, Pallas kernels for 15%

profile of v2, /device:TPU:1, one launch (start us, length us, event | category | flops | bytes accessed | tf_op | source)
XLA Modules:
  0.0 147.1 jit_solution(16141690266824883217)
XLA Ops:
  7.2 0.0 all-gather.3.cloned.1.call-start
  7.9 0.1 pad_add_fusion.place_ref
  7.9 2.8 %shard_map.85 = (bf16[1280,384]{1,0:T(8,128)(2,1)S(1)}, bf16[256,384]{1,0:T(8,128)(2,1)}) custom-call(s32[3]{0:T(128)S(1)} %pad_add_fusion.place_ref, bf16[256,384]{1,0:T(8,128)(2,1)} %new_hbm.1, bf16[768,384]{1,0:T(8,128)(2,1)} %queue_hbm.3, bf16[256,384]{1,0:T(8,128)(2,1)} %student_hbm.1), custom_call_target="tpu_custom_call" | custom-call | flops 3932160 | tf_op jit(solution)/shard_map/pallas_call | solution.py:37
  10.8 0.0 all-gather.3.cloned.1.call-update
  10.8 0.0 copy-start
  10.8 6.3 %shard_map.86 = (f32[1024,2048]{1,0:T(8,128)S(1)}, f32[256,2048]{1,0:T(8,128)S(1)}, f32[1,2048]{1,0:T(1,128)S(1)}, f32[1,256]{1,0:T(1,128)S(1)}) custom-call(bf16[1280,384]{1,0:T(8,128)(2,1)S(1)} %get-tuple-element.16.hat, bf16[2048,384]{1,0:T(8,128)(2,1)} %proto_hbm.3), custom_call_target="tpu_custom_call" | custom-call | flops 2013265920 | tf_op jit(solution)/shard_map/pallas_call | solution.py:37
  17.1 0.0 copy-done
  17.2 18.1 %all_to_all.35.first_ref = f32[8,1,2304]{2,1,0:T(1,128)S(1)} all-to-all(f32[8,1,2304]{2,1,0:T(1,128)S(1)} %broadcast_in_dim.49), channel_id=1, replica_groups=mesh['proto_0'=8,'proto_1'=4,'proto_2'=2,'sample'=8] {'sample'}, dimensions={0} | all-to-all | bytes 147456 | tf_op jit(solution)/shard_map/all_to_all | solution.py:309
  35.3 0.1 fusion.2
  35.4 1.2 shard_map.87
  36.6 0.2 broadcast_in_dim.51
  36.8 26.1 %all_to_all.36 = f32[64,1,1280]{2,1,0:T(1,128)S(1)} all-to-all(f32[64,1,1280]{2,1,0:T(1,128)S(1)} %broadcast_in_dim.51), channel_id=1, replica_groups=mesh['proto_0'=8,'proto_1'=4,'proto_2'=2,'sample'=8] {'proto_0','proto_1..., dimensions={0} | all-to-all | bytes 655360 | tf_op jit(solution)/shard_map/all_to_all | solution.py:309
  63.0 0.1 fusion
  63.1 1.2 shard_map.88
  64.3 0.1 slice_reduce_fusion
  64.4 9.8 %all_to_all.37.second_ref = f32[8,1,2304]{2,1,0:T(1,128)S(1)} all-to-all(f32[8,1,2304]{2,1,0:T(1,128)S(1)} %broadcast_in_dim.53), channel_id=1, replica_groups=mesh['proto_0'=8,'proto_1'=4,'proto_2'=2,'sample'=8] {'sample'}, dimensions={0} | all-to-all | bytes 147456 | tf_op jit(solution)/shard_map/all_to_all | solution.py:309
  74.2 0.1 fusion.3
  74.3 1.2 shard_map.89
  75.5 0.1 broadcast_in_dim.55
  75.6 19.0 %all_to_all.38 = f32[64,1,1024]{2,1,0:T(1,128)S(1)} all-to-all(f32[64,1,1024]{2,1,0:T(1,128)S(1)} %broadcast_in_dim.55), channel_id=1, replica_groups=mesh['proto_0'=8,'proto_1'=4,'proto_2'=2,'sample'=8] {'proto_0','proto_1..., dimensions={0} | all-to-all | bytes 524288 | tf_op jit(solution)/shard_map/all_to_all | solution.py:309
  94.6 0.1 fusion.1
  94.7 1.2 shard_map.90
  95.9 9.5 %all_to_all.39 = f32[8,1,2048]{2,1,0:T(1,128)S(1)} all-to-all(f32[8,1,2048]{2,1,0:T(1,128)S(1)} %broadcast_in_dim.57), channel_id=1, replica_groups=mesh['proto_0'=8,'proto_1'=4,'proto_2'=2,'sample'=8] {'sample'}, dimensions={0} | all-to-all | bytes 131072 | tf_op jit(solution)/shard_map/all_to_all | solution.py:309
  105.4 0.1 multiply_reduce_fusion
  105.5 0.4 shard_map.92
  105.9 0.1 broadcast_in_dim.59
  106.0 16.9 %all_to_all.40.got_ref = f32[64,1,512]{2,1,0:T(1,128)S(1)} all-to-all(f32[64,1,512]{2,1,0:T(1,128)S(1)} %broadcast_in_dim.59), channel_id=1, replica_groups=mesh['proto_0'=8,'proto_1'=4,'proto_2'=2,'sample'=8] {'proto_0','proto_1..., dimensions={0} | all-to-all | bytes 262144 | tf_op jit(solution)/shard_map/all_to_all | solution.py:309
  122.9 0.8 shard_map.93
  123.7 3.3 %all-to-all-start.6 = ((f32[8,1,384]{2,1,0:T(1,128)}), f32[8,1,384]{2,1,0:T(1,128)S(1)}, u32[]{:S(2)}, u32[]{:S(2)}) async-start(f32[8,1,384]{2,1,0:T(1,128)} %shard_map.93), calls=%async_computation.6 | async-start | bytes 24576 | tf_op jit(solution)/shard_map/all_to_all | solution.py:402
  127.0 0.0 all-gather.3.cloned.1.call-done
  127.0 9.6 %shard_map.91 = (f32[256,2048]{1,0:T(8,128)S(1)}, f32[256,2048]{1,0:T(8,128)}, f32[256,384]{1,0:T(8,128)S(1)}, f32[256,1]{1,0:T(8,128)S(1)}, bf16[768,384]{1,0:T(8,128)(2,1)}) custom-call(s32[3]{0:T(128)S(1)} %pad_add_fusion.place_ref, f32[8,1,2304]{2,1,0:T(1,128)S(1)} %all_to_all.35.first_ref, f32[8,1,2304]{2,1,0:T(1,128)S(1)} %all_to_all.37.second_ref, ...), custom_call_target="tpu_custom_call" | custom-call | flops 805306368 | tf_op jit(solution)/shard_map/pallas_call | solution.py:37
  136.6 0.0 all-to-all-done.6.got_ref
  136.6 3.6 %shard_map.94 = (f32[256,384]{1,0:T(8,128)}, f32[1,1]{1,0:T(1,128)}) custom-call(f32[8,1,384]{2,1,0:T(1,128)S(1)} %all-to-all-done.6.got_ref, f32[256,2048]{1,0:T(8,128)S(1)} %get-tuple-element.23.scores_ref, f32[256,2048]{1,0:T(8,128)} %get-tuple-element.24.soft_hbm, bf16[16,256,384]{2,1,0:T(8,128)(2,1)} %bitcast.27, ...), custom_call_target="tpu_custom_call" | custom-call | flops 402653184 | tf_op jit(solution)/shard_map/pallas_call | solution.py:37
  (13 shorter events, 0.2 us)
Async XLA Ops:
  7.2 119.8 %all-gather.3.cloned.1.call-start = ((), (), s32[]{:S(2)}) async-start(), calls=%async_computation.7 | async-start | bytes 3342336 | tf_op jit(solution)/shard_map/all_gather | solution.py:348
  10.8 6.4 %copy-start = (s32[256,1]{0,1:T(1,128)S(1)}, s32[256,1]{0,1:T(1,128)}, u32[]{:S(2)}) copy-start(s32[256,1]{0,1:T(1,128)} %param.10) | copy-start | bytes 3076
  123.7 13.0 %all-to-all-start.6 = ((f32[8,1,384]{2,1,0:T(1,128)}), f32[8,1,384]{2,1,0:T(1,128)S(1)}, u32[]{:S(2)}, u32[]{:S(2)}) async-start(f32[8,1,384]{2,1,0:T(1,128)} %shard_map.93), calls=%async_computation.6 | async-start | bytes 24576 | tf_op jit(solution)/shard_map/all_to_all | solution.py:402
Sparse Core Ops, SparseCore 0:
  10.9 50.2 all-gather.2

commit v3 on v2

--- a/solution.py
+++ b/solution.py
@@ -101,85 +101,112 @@
 
 
 def scores_body(
-    hat, proto_hbm, scores_ref, cross_ref, sums_ref, partial_ref, raw_proto, total, proto_sems
+    hat, owner_ref, proto_hbm,
+    scores_ref, cross_ref, message_ref, partial_ref,
+    raw_proto, product_even, product_odd, total, sums, proto_sems,
 ):
     def proto_copy(turn):
-        rows = pl.ds(pl.multiple_of(turn * 256, 256), 256)
+        rows = pl.ds(turn * 256, 256)
         return pltpu.make_async_copy(proto_hbm.at[rows], raw_proto.at[rows], proto_sems.at[turn])
 
-    for turn in range(K_DEV // 256):
-        proto_copy(turn).start()
+    n_tiles = K_DEV // 256
+    copies = [proto_copy(turn) for turn in range(n_tiles)]
+    for copy in copies:
+        copy.start()
     total[...] = jnp.zeros_like(total)
-
-    def tile(turn, carry):
-        start = pl.multiple_of(turn * 256, 256)
-        rows = pl.ds(start, 256)
-        proto_copy(turn).wait()
-        proto = unit_rows(raw_proto[rows, :])[0].astype(BF16)
+    sums[...] = jnp.zeros_like(sums)
+    sums[K_DEV // 128 : K_DEV // 128 + 2] = owner_ref[...].astype(F32)
+    buffers = (product_even, product_odd)
+
+    def multiply(turn):
+        copies[turn].wait()
+        proto = unit_rows(raw_proto[turn * 256 : turn * 256 + 256])[0].astype(BF16)
+        buffers[turn % 2][...] = against(hat[...], proto)
+
+    def finish(turn):
+        product = buffers[turn % 2]
+        lanes = slice(turn * 256, turn * 256 + 256)
         column = jnp.zeros((8, 256), F32)
-        for part in range(ROWS // 256):
-            span = slice(part * 256, part * 256 + 256)
-            scores = jnp.exp2(against(hat[span], proto) * TEACHER_EXP2)
-            scores_ref[span, rows] = scores
-            column += jnp.sum(scores.reshape(32, 8, 256), axis=0)
-        sums_ref[:, rows] = jnp.sum(column, axis=0, keepdims=True)
-        product = against(hat[ROWS:], proto)
-        cross_ref[:, rows] = scores_ref[:NEW_DEV, rows] * (product * (1.0 / student_temp))
-        exped = jnp.exp2(product * STUDENT_EXP2)
-        total[...] += exped[:, :128] + exped[:, 128:]
-        return carry
-
-    lax.fori_loop(0, K_DEV // 256, tile, 0)
+        for start in range(0, ROWS, 64):
+            rows = slice(start, start + 64)
+            scores = jnp.exp2(product[rows] * TEACHER_EXP2)
+            scores_ref[rows, lanes] = scores
+            column += jnp.sum(scores.reshape(8, 8, 256), axis=0)
+            if start < NEW_DEV:
+                logits = product[ROWS + start : ROWS + start + 64]
+                cross_ref[rows, lanes] = scores * (logits * (1.0 / student_temp))
+                exped = jnp.exp2(logits * STUDENT_EXP2)
+                total[rows] += exped[:, :128] + exped[:, 128:]
+        column = jnp.sum(column, axis=0, keepdims=True)
+        sums[2 * turn : 2 * turn + 1] = column[:, :128]
+        sums[2 * turn + 1 : 2 * turn + 2] = column[:, 128:]
+
+    multiply(0)
+    for turn in range(n_tiles):
+        if turn + 1 < n_tiles:
+            multiply(turn + 1)
+        finish(turn)
     for part in range(NEW_DEV // 128):
-        span = slice(part * 128, part * 128 + 128)
-        partial_ref[:, span] = lane_sums(total[span])
-
-
-def weigh_columns(source_ref, row, out_ref, span, block):
-    def chunk(turn):
-        lanes = slice(turn * 128, turn * 128 + 128)
-        return source_ref[block, lanes] * row[:, lanes]
-
-    total = chunk(0)
-    for turn in range(1, K_DEV // 128):
-        total += chunk(turn)
-    out_ref[:, span] = lane_sums(total)
-
-
-def row_totals_body(scores_ref, weight_ref, out_ref):
-    row = weight_ref[...]
-
-    def block(turn, carry):
-        start = pl.multiple_of(turn * 128, 128)
-        weigh_columns(scores_ref, row, out_ref, pl.ds(start, 128), pl.ds(start, 128))
-        return carry
-
-    lax.fori_loop(0, ROWS // 128, block, 0)
-
-
-def last_totals_body(scores_ref, cross_ref, weight_ref, out_ref):
-    row = weight_ref[...]
+        partial_ref[part : part + 1] = lane_sums(total[part * 128 : part * 128 + 128])
+    message = sums[...].astype(BF16)
+    for peer in range(message_ref.shape[0]):
+        message_ref[peer] = message
+
+
+def received(got_ref, n_rows):
+    total = got_ref[0, :n_rows].astype(F32)
+    for peer in range(1, got_ref.shape[0]):
+        total += got_ref[peer, :n_rows].astype(F32)
+    return total
+
+
+def weigh_columns(source_ref, scale_ref, block):
+    total = None
+    for turn in range(K_DEV // 128):
+        part = source_ref[block, turn * 128 : turn * 128 + 128] * scale_ref[turn : turn + 1]
+        total = part if turn == 0 else total + part
+    return lane_sums(total)
+
+
+def row_totals_body(factor, got_ref, scores_ref, message_ref, scale, totals):
+    scale[...] = 1.0 / (received(got_ref, K_DEV // 128) * factor)
+    for part in range(ROWS // 128):
+        block = slice(part * 128, part * 128 + 128)
+        totals[part : part + 1] = weigh_columns(scores_ref, scale, block)
+    message = totals[...].astype(message_ref.dtype)
+    for peer in range(message_ref.shape[0]):
+        message_ref[peer] = message
+
+
+def last_totals_body(
+    factor, got_ref, scores_ref, cross_ref, partial_ref, message_ref, scale_ref
+):
+    scale_ref[...] = 1.0 / (received(got_ref, K_DEV // 128) * factor)
+    rows = []
+    for source in (scores_ref, cross_ref):
+        for part in range(NEW_DEV // 128):
+            block = slice(part * 128, part * 128 + 128)
+            rows.append(weigh_columns(source, scale_ref, block))
     for part in range(NEW_DEV // 128):
-        block = slice(part * 128, part * 128 + 128)
-        weigh_columns(scores_ref, row, out_ref, block, block)
-        span = slice(NEW_DEV + part * 128, NEW_DEV + part * 128 + 128)
-        weigh_columns(cross_ref, row, out_ref, span, block)
-
-
-def column_sums_body(scores_ref, weight_ref, out_ref, total):
-    total[...] = jnp.zeros_like(total)
-
-    def block(turn, carry):
-        start = pl.multiple_of(turn * 128, 128)
-        weights = along_rows(weight_ref[:, pl.ds(start, 128)])
-        for chunk in range(K_DEV // 128):
-            lanes = slice(chunk * 128, chunk * 128 + 128)
-            part = scores_ref[pl.ds(start, 128), lanes] * weights
-            total[:, lanes] += jnp.sum(part.reshape(16, 8, 128), axis=0)
-        return carry
-
-    lax.fori_loop(0, ROWS // 128, block, 0)
-    out_ref[...] = jnp.sum(total[...], axis=0, keepdims=True)
+        rows.append(partial_ref[part : part + 1])
+    message_ref[...] = jnp.broadcast_to(jnp.concatenate(rows, axis=1)[None], message_ref.shape)
+
+
+def column_sums_body(factor, got_ref, scores_ref, message_ref, weights, sums):
+    scale = 1.0 / (received(got_ref, ROWS // 128) * factor)
+    for part in range(ROWS // 128):
+        weights[part * 128 : part * 128 + 128] = along_rows(scale[part : part + 1])
+    for chunk in range(K_DEV // 128):
+        lanes = slice(chunk * 128, chunk * 128 + 128)
+        total = jnp.zeros((8, 128), F32)
+        for start in range(0, ROWS, 64):
+            rows = slice(start, start + 64)
+            part = scores_ref[rows, lanes] * weights[rows]
+            total += jnp.sum(part.reshape(8, 8, 128), axis=0)
+        sums[chunk : chunk + 1] = jnp.sum(total, axis=0, keepdims=True)
+    message = sums[...].astype(message_ref.dtype)
+    for peer in range(message_ref.shape[0]):
+        message_ref[peer] = message
 
 
 def message_lanes(chunk):
@@ -187,7 +214,7 @@
 
 
 def gathered_body(
-    factor, place_ref, first_ref, second_ref, everyone_hbm, queue_hbm, proto_hbm, column_ref,
+    factor, place_ref, first_ref, everyone_hbm, queue_hbm, proto_hbm, scale_ref,
     scores_ref, soft_hbm, unit_ref, length_ref, out_ref,
     rows_in, proto_in, queue_in, soft, chosen, row_sems, soft_sems, proto_sem, queue_sem,
 ):
@@ -211,7 +238,7 @@
     queue_copy = pltpu.make_async_copy(queue_hbm, queue_in, queue_sem)
     queue_copy.start()
     columns = [
-        along_rows(column_ref[:, pl.ds(pl.multiple_of(first + part * 128, 128), 128)] * factor)
+        along_rows(scale_ref[pl.ds(place_ref[0] * 2 + part, 1), :] * factor)
         for part in range(share // 128)
     ]
     proto_copy.wait()
@@ -226,8 +253,7 @@
         for side in range(2):
             lanes = pl.ds(pl.multiple_of(start + side * 128, 128), 128)
             exped = jnp.exp2(against(proto, rows_in[turn * 2 + side, :128, :]) * STUDENT_EXP2)
-            names = slice(K_DEV + side * 128, K_DEV + side * 128 + 128)
-            soft[:, lanes] = exped * (factor / second_ref[turn, :, names])
+            soft[:, lanes] = exped
             teacher = unit_rows(rows_in[turn * 2 + side, 128:, :])[0].astype(BF16)
             scores = jnp.exp2(against(proto, teacher) * TEACHER_EXP2)
             for part in range(2):
@@ -247,9 +273,8 @@
     slots = lax.broadcasted_iota(jnp.int32, (QUEUE_PER_INDEX, 128), 0).astype(F32)
     base = jnp.zeros((1, 1), F32)
     for chunk in range(n_new // 128):
-        plane, lanes = message_lanes(chunk)
-        names = slice(K_DEV + lanes.start, K_DEV + lanes.stop)
-        named = jnp.where(first_ref[plane, :, names] == mine, 1.0, 0.0)
+        names = first_ref[chunk // 2, K_DEV // 128 : K_DEV // 128 + 8].astype(F32)
+        named = jnp.where(names[chunk % 2 : chunk % 2 + 1] == mine, 1.0, 0.0)
         ahead = jnp.dot(
             jnp.broadcast_to(named, (16, 128)).astype(BF16), before, preferred_element_type=F32
         )[:1]
@@ -268,45 +293,65 @@
         soft_copy(turn).wait()
 
 
-def rows_body(got_ref, denominator_ref, out_ref):
+def rows_body(got_ref, out_ref):
     totals = jnp.sum(got_ref[...], axis=0)
     row_scale = 1.0 / totals[:, :NEW_DEV]
-    terms = jnp.log(denominator_ref[...]) - row_scale * totals[:, NEW_DEV:]
+    denominator = totals[:, 2 * NEW_DEV :]
+    terms = jnp.log(denominator) - row_scale * totals[:, NEW_DEV : 2 * NEW_DEV]
     loss = jnp.broadcast_to(jnp.sum(terms, axis=1, keepdims=True), (1, 128))
-    message = jnp.concatenate([row_scale, loss], axis=1)
+    message = jnp.concatenate([row_scale, denominator, loss], axis=1)
     out_ref[...] = jnp.broadcast_to(message[None], out_ref.shape)
 
 
 def gradient_body(
-    got_ref, scores_ref, soft_hbm, everyone_hbm, unit_ref, length_ref, out_ref, loss_ref,
-    soft, student, gradient, soft_sem, student_sem,
+    factor, got_ref, scores_ref, soft_hbm, everyone_hbm, unit_ref, length_ref, out_ref, loss_ref,
+    soft, student, gradient, soft_sems, student_sems,
 ):
     n_blocks = student.shape[0]
     n_new = n_blocks * 128
-    soft_copy = pltpu.make_async_copy(soft_hbm, soft, soft_sem)
-    student_copy = pltpu.make_async_copy(
-        everyone_hbm.at[:, pl.ds(0, 128), :], student, student_sem
-    )
-    soft_copy.start()
-    student_copy.start()
-    loss_ref[...] = jnp.sum(got_ref[:, :, NEW_DEV : NEW_DEV + 1], axis=0) * (1.0 / n_new)
-    soft_copy.wait()
-    for chunk in range(n_blocks):
-        plane, names = message_lanes(chunk)
-        lanes = slice(chunk * 128, chunk * 128 + 128)
-        target = scores_ref[:, lanes] * got_ref[plane, :, names]
-        gradient[:, lanes] = (soft[:, lanes] - target).astype(BF16)
-    student_copy.wait()
-    students = student[...].reshape(n_new, FEATURE_WIDTH)
-    unit_gradient = jnp.dot(gradient[...], students, preferred_element_type=F32)
+    n_parts = soft_sems.shape[0]
+    step = n_blocks // n_parts
+    soft_copies, student_copies = [], []
+    for part in range(n_parts):
+        lanes = pl.ds(part * step * 128, step * 128)
+        soft_copies.append(
+            pltpu.make_async_copy(soft_hbm.at[:, lanes], soft.at[:, lanes], soft_sems.at[part])
+        )
+        blocks = pl.ds(part * step, step)
+        student_copies.append(
+            pltpu.make_async_copy(
+                everyone_hbm.at[blocks, pl.ds(0, 128), :], student.at[blocks], student_sems.at[part]
+            )
+        )
+        soft_copies[part].start()
+        student_copies[part].start()
+    loss_at = 2 * NEW_DEV
+    loss_ref[...] = jnp.sum(got_ref[:, :, loss_at : loss_at + 1], axis=0) * (1.0 / n_new)
+    unit_gradient = None
+    for part in range(n_parts):
+        soft_copies[part].wait()
+        for chunk in range(part * step, part * step + step):
+            plane, names = message_lanes(chunk)
+            others = slice(NEW_DEV + names.start, NEW_DEV + names.stop)
+            lanes = slice(chunk * 128, chunk * 128 + 128)
+            value = soft[:, lanes] * (factor / got_ref[plane, :, others])
+            target = scores_ref[:, lanes] * got_ref[plane, :, names]
+            gradient[:, lanes] = (value - target).astype(BF16)
+        student_copies[part].wait()
+        students = student[part * step : part * step + step].reshape(step * 128, FEATURE_WIDTH)
+        piece = jnp.dot(
+            gradient[:, part * step * 128 : (part + 1) * step * 128],
+            students,
+            preferred_element_type=F32,
+        )
+        unit_gradient = piece if part == 0 else unit_gradient + piece
     unit = unit_ref[...]
     along = jnp.sum(unit * unit_gradient, axis=1, keepdims=True)
     out_ref[...] = (unit_gradient - unit * along) / length_ref[...]
 
 
-def from_everyone(row, axis):
-    copies = jnp.broadcast_to(row[None], (lax.axis_size(axis), *row.shape))
-    return lax.all_to_all(copies, axis, split_axis=0, concat_axis=0, tiled=True)
+def exchange(message, axis):
+    return lax.all_to_all(message, axis, split_axis=0, concat_axis=0, tiled=True)
 
 
 def on_device(teacher_new, queue, student, prototypes, owners, queue_oldest_slot):
@@ -346,60 +391,61 @@
         out_specs=(VMEM, HBM),
     )
     everyone = lax.all_gather(half, ("sample", "proto_2"), axis=0)
-    scores, cross, sums, partial = call(
+    scores, cross, message, partial = call(
         scores_body,
-        (shape((ROWS, K_DEV)), shape((NEW_DEV, K_DEV)), shape((1, K_DEV)), shape((1, NEW_DEV))),
-        (hat, in_hbm(prototypes)),
-        8,
+        (
+            shape((ROWS, K_DEV)),
+            shape((NEW_DEV, K_DEV)),
+            shape((n_sample, K_DEV // 128 + 8, 128), BF16),
+            shape((NEW_DEV // 128, 128)),
+        ),
+        (hat, owners.reshape(NEW_DEV // 128, 128), in_hbm(prototypes)),
+        10,
         2 * (ROWS + NEW_DEV) * K_DEV * FEATURE_WIDTH,
         [
             pltpu.VMEM((K_DEV, FEATURE_WIDTH), BF16),
+            pltpu.VMEM((ROWS + NEW_DEV, 256), F32),
+            pltpu.VMEM((ROWS + NEW_DEV, 256), F32),
             pltpu.VMEM((NEW_DEV, 128), F32),
+            pltpu.VMEM((K_DEV // 128 + 8, 128), F32),
             DMA((K_DEV // 256,)),
         ],
-        in_specs=[VMEM, HBM],
-    )
-    owner_row = owners.reshape(1, NEW_DEV).astype(F32)
-    first = from_everyone(jnp.concatenate([sums, owner_row], axis=1), "sample")
-    proto_scale = 1.0 / jnp.sum(first[:, :, :K_DEV] * protos_total, axis=0)
-
-    denominator = None
-    second = None
+        in_specs=[VMEM, VMEM, HBM],
+    )
+    first = got = exchange(message, "sample")
     for iteration in range(ITERS - 1):
-        totals = call(row_totals_body, shape((1, ROWS)), (scores, proto_scale), 4, 2 * ROWS * K_DEV)
-        if iteration == 0:
-            totals = jnp.concatenate([totals, partial], axis=1)
-        got = from_everyone(totals, PROTO)
-        if iteration == 0:
-            denominator = jnp.sum(got[:, :, ROWS:], axis=0)
-        row_scale = 1.0 / jnp.sum(got[:, :, :ROWS] * teachers_total, axis=0)
-        sums = call(
-            column_sums_body,
-            shape((1, K_DEV)),
-            (scores, row_scale),
+        message = call(
+            functools.partial(row_totals_body, protos_total),
+            shape((n_proto, ROWS // 128, 128), BF16),
+            (got, scores),
             4,
             2 * ROWS * K_DEV,
-            [pltpu.VMEM((8, K_DEV), F32)],
+            [pltpu.VMEM((K_DEV // 128, 128), F32), pltpu.VMEM((ROWS // 128, 128), F32)],
         )
-        if iteration == 0:
-            sums = jnp.concatenate([sums, denominator], axis=1)
-        got = from_everyone(sums, "sample")
-        if iteration == 0:
-            second = got
-        proto_scale = 1.0 / jnp.sum(got[:, :, :K_DEV] * protos_total, axis=0)
-
-    totals = call(
-        last_totals_body,
-        shape((1, 2 * NEW_DEV)),
-        (scores, cross, proto_scale),
+        got = exchange(message, PROTO)
+        wide = iteration == ITERS - 2
+        message = call(
+            functools.partial(column_sums_body, teachers_total),
+            shape((n_sample, K_DEV // 128, 128), F32 if wide else BF16),
+            (got, scores),
+            4,
+            2 * ROWS * K_DEV,
+            [pltpu.VMEM((ROWS, 128), F32), pltpu.VMEM((K_DEV // 128, 128), F32)],
+        )
+        got = exchange(message, "sample")
+
+    message, proto_scale = call(
+        functools.partial(last_totals_body, protos_total),
+        (shape((n_proto, 1, 3 * NEW_DEV)), shape((K_DEV // 128, 128))),
+        (got, scores, cross, partial),
         4,
         4 * NEW_DEV * K_DEV,
     )
-    got = from_everyone(totals, PROTO)
+    got = exchange(message, PROTO)
     message = call(
-        rows_body, shape((n_sample, 1, NEW_DEV + 128)), (got, denominator), 4, n_proto * 2 * NEW_DEV
-    )
-    got = lax.all_to_all(message, "sample", split_axis=0, concat_axis=0, tiled=True)
+        rows_body, shape((n_sample, 1, 2 * NEW_DEV + 128)), (got,), 4, n_proto * 3 * NEW_DEV
+    )
+    got = exchange(message, "sample")
 
     all_scores, all_soft, my_unit, my_length, new_queue = call(
         functools.partial(gathered_body, factor),
@@ -410,7 +456,7 @@
             shape((share, 1)),
             shape((QUEUE_PER_INDEX, FEATURE_WIDTH), BF16),
         ),
-        (place, first, second, in_hbm(everyone), in_hbm(queue), in_hbm(prototypes), proto_scale),
+        (place, first, in_hbm(everyone), in_hbm(queue), in_hbm(prototypes), proto_scale),
         16,
         4 * share * new_total * FEATURE_WIDTH,
         [
@@ -424,11 +470,11 @@
             DMA,
             DMA,
         ],
-        in_specs=[SMEM, VMEM, VMEM, HBM, HBM, HBM, VMEM],
+        in_specs=[SMEM, VMEM, HBM, HBM, HBM, VMEM],
         out_specs=(VMEM, HBM, VMEM, VMEM, VMEM),
     )
     proto_grad, loss = call(
-        gradient_body,
+        functools.partial(gradient_body, factor),
         (shape((share, FEATURE_WIDTH)), shape((1, 1))),
         (got, all_scores, in_hbm(all_soft), in_hbm(everyone), my_unit, my_length),
         12,
@@ -437,8 +483,8 @@
             pltpu.VMEM((share, new_total), F32),
             pltpu.VMEM((new_total // 128, 128, FEATURE_WIDTH), BF16),
             pltpu.VMEM((share, new_total), BF16),
-            DMA,
-            DMA,
+            DMA((4,)),
+            DMA((4,)),
         ],
         in_specs=[VMEM, VMEM, HBM, HBM, VMEM, VMEM],
     )

time: 148 us -> 142 us (0.959)
  blocking collectives: 99.4 us -> 93.3 us
    all_to_all x6, blocking collectives: 99.4 us -> 93.3 us  [exchange(): lax.all_to_all(message, axis, split_axis=0, concat_axis=0, tiled=True)]
  transfers between devices with their start and end apart: 2 -> 2, of which waited for: 0 -> 0; matrix products, arithmetic and copies ran while one was open for 1% -> 0% of each run, Pallas kernels for 15% -> 16%
where the time goes in v3:
time: 142 us
  blocking collectives  93.3 us (66%)
  Pallas kernels  29.5 us (21%)
  between operations  14.8 us (10%)
  starting transfers between devices  3.37 us (2%)
    all_to_all x6, blocking collectives, exchange(): lax.all_to_all(message, axis, split_axis=0, concat_axis=0, tiled=True)  93.3 us
    pallas_call x10, Pallas kernels, call(): pl.pallas_call(body, out_shape=out_shape, in_specs=in_specs or [VMEM] * l...  29.5 us
    all_to_all x1, starting transfers between devices, exchange(): lax.all_to_all(message, axis, split_axis=0, concat_axis=0, tiled=True)  3.33 us
  transfers between devices with their start and end apart: 2, of which 0 were waited for; matrix products, arithmetic and copies ran while one was open for 0% of the time, Pallas kernels for 16%

profile of v3, /device:TPU:1, one launch (start us, length us, event | category | flops | bytes accessed | tf_op | source)
XLA Modules:
  0.0 141.8 jit_solution(12363596317233373694)
XLA Ops:
  7.2 0.0 all-gather.3.cloned.1.call-start
  7.9 0.1 pad_add_fusion.place_ref
  7.9 2.8 %shard_map.85 = (bf16[1280,384]{1,0:T(8,128)(2,1)S(1)}, bf16[256,384]{1,0:T(8,128)(2,1)}) custom-call(s32[3]{0:T(128)S(1)} %pad_add_fusion.place_ref, bf16[256,384]{1,0:T(8,128)(2,1)} %new_hbm.1, bf16[768,384]{1,0:T(8,128)(2,1)} %queue_hbm.3, bf16[256,384]{1,0:T(8,128)(2,1)} %student_hbm.1), custom_call_target="tpu_custom_call" | custom-call | flops 3932160 | tf_op jit(solution)/shard_map/pallas_call | solution.py:37
  10.8 0.0 all-gather.3.cloned.1.call-update
  10.8 0.0 copy-start
  10.8 0.7 copy-done
  11.5 9.6 %shard_map.86 = (f32[1024,2048]{1,0:T(8,128)S(1)}, f32[256,2048]{1,0:T(8,128)S(1)}, bf16[8,24,128]{2,1,0:T(8,128)(2,1)S(1)}, f32[2,128]{1,0:T(2,128)S(1)}) custom-call(bf16[1280,384]{1,0:T(8,128)(2,1)S(1)} %get-tuple-element.18.hat, s32[2,128]{1,0:T(2,128)S(1)} %bitcast.5, bf16[2048,384]{1,0:T(8,128)(2,1)} %proto_hbm.3), custom_call_target="tpu_custom_call" | custom-call | flops 2013265920 | tf_op jit(solution)/shard_map/pallas_call | solution.py:37
  21.1 18.1 %all_to_all.35.got_ref.first_ref = bf16[8,24,128]{2,1,0:T(8,128)(2,1)S(1)} all-to-all(bf16[8,24,128]{2,1,0:T(8,128)(2,1)S(1)} %get-tuple-element.19), channel_id=1, replica_groups=mesh['proto_0'=8,'proto_1'=4,'proto_2'=2,'sample'=8] {'sample'}, dimensions={0} | all-to-all | bytes 98304 | tf_op jit(solution)/shard_map/all_to_all | solution.py:354
  39.2 0.7 shard_map.87
  39.9 23.1 %all_to_all.36.got_ref = bf16[64,8,128]{2,1,0:T(8,128)(2,1)S(1)} all-to-all(bf16[64,8,128]{2,1,0:T(8,128)(2,1)S(1)} %shard_map.87), channel_id=1, replica_groups=mesh['proto_0'=8,'proto_1'=4,'proto_2'=2,'sample'=8] {'proto_0','proto_1..., dimensions={0} | all-to-all | bytes 262144 | tf_op jit(solution)/shard_map/all_to_all | solution.py:354
  63.0 0.8 shard_map.88
  63.8 9.2 %all_to_all.37.got_ref = bf16[8,16,128]{2,1,0:T(8,128)(2,1)S(1)} all-to-all(bf16[8,16,128]{2,1,0:T(8,128)(2,1)S(1)} %shard_map.88), channel_id=1, replica_groups=mesh['proto_0'=8,'proto_1'=4,'proto_2'=2,'sample'=8] {'sample'}, dimensions={0} | all-to-all | bytes 65536 | tf_op jit(solution)/shard_map/all_to_all | solution.py:354
  73.0 0.7 shard_map.89
  73.7 16.0 %all_to_all.38.got_ref = bf16[64,8,128]{2,1,0:T(8,128)(2,1)S(1)} all-to-all(bf16[64,8,128]{2,1,0:T(8,128)(2,1)S(1)} %shard_map.89), channel_id=1, replica_groups=mesh['proto_0'=8,'proto_1'=4,'proto_2'=2,'sample'=8] {'proto_0','proto_1..., dimensions={0} | all-to-all | bytes 262144 | tf_op jit(solution)/shard_map/all_to_all | solution.py:354
  89.8 0.8 shard_map.90
  90.5 9.5 %all_to_all.39.got_ref = f32[8,16,128]{2,1,0:T(8,128)S(1)} all-to-all(f32[8,16,128]{2,1,0:T(8,128)S(1)} %shard_map.90), channel_id=1, replica_groups=mesh['proto_0'=8,'proto_1'=4,'proto_2'=2,'sample'=8] {'sample'}, dimensions={0} | all-to-all | bytes 131072 | tf_op jit(solution)/shard_map/all_to_all | solution.py:354
  100.1 0.4 shard_map.91
  100.5 17.2 %all_to_all.40.got_ref = f32[64,1,768]{2,1,0:T(1,128)S(1)} all-to-all(f32[64,1,768]{2,1,0:T(1,128)S(1)} %get-tuple-element.26), channel_id=1, replica_groups=mesh['proto_0'=8,'proto_1'=4,'proto_2'=2,'sample'=8] {'proto_0','proto_1..., dimensions={0} | all-to-all | bytes 393216 | tf_op jit(solution)/shard_map/all_to_all | solution.py:354
  117.7 0.8 shard_map.93
  118.5 3.3 %all-to-all-start.6 = ((f32[8,1,640]{2,1,0:T(1,128)}), f32[8,1,640]{2,1,0:T(1,128)S(1)}, u32[]{:S(2)}, u32[]{:S(2)}) async-start(f32[8,1,640]{2,1,0:T(1,128)} %shard_map.93), calls=%async_computation.6 | async-start | bytes 40960 | tf_op jit(solution)/shard_map/all_to_all | solution.py:354
  121.8 0.0 all-gather.3.cloned.1.call-done
  121.9 9.4 %shard_map.92 = (f32[256,2048]{1,0:T(8,128)S(1)}, f32[256,2048]{1,0:T(8,128)}, f32[256,384]{1,0:T(8,128)S(1)}, f32[256,1]{1,0:T(8,128)S(1)}, bf16[768,384]{1,0:T(8,128)(2,1)}) custom-call(s32[3]{0:T(128)S(1)} %pad_add_fusion.place_ref, bf16[8,24,128]{2,1,0:T(8,128)(2,1)S(1)} %all_to_all.35.got_ref.first_ref, bf16[16,256,384]{2,1,0:T(8,128)(2,1)} %bitcast.6, ...), custom_call_target="tpu_custom_call" | custom-call | flops 805306368 | tf_op jit(solution)/shard_map/pallas_call | solution.py:37
  131.3 0.0 all-to-all-done.6.got_ref
  131.3 3.6 %shard_map.94 = (f32[256,384]{1,0:T(8,128)}, f32[1,1]{1,0:T(1,128)}) custom-call(f32[8,1,640]{2,1,0:T(1,128)S(1)} %all-to-all-done.6.got_ref, f32[256,2048]{1,0:T(8,128)S(1)} %get-tuple-element.27.scores_ref, f32[256,2048]{1,0:T(8,128)} %get-tuple-element.28.soft_hbm, bf16[16,256,384]{2,1,0:T(8,128)(2,1)} %bitcast.7, ...), custom_call_target="tpu_custom_call" | custom-call | flops 402653184 | tf_op jit(solution)/shard_map/pallas_call | solution.py:37
Async XLA Ops:
  7.2 114.7 %all-gather.3.cloned.1.call-start = ((), (), s32[]{:S(2)}) async-start(), calls=%async_computation.7 | async-start | bytes 3342336 | tf_op jit(solution)/shard_map/all_gather | solution.py:393
  10.8 0.7 copy-start
  118.5 12.8 %all-to-all-start.6 = ((f32[8,1,640]{2,1,0:T(1,128)}), f32[8,1,640]{2,1,0:T(1,128)S(1)}, u32[]{:S(2)}, u32[]{:S(2)}) async-start(f32[8,1,640]{2,1,0:T(1,128)} %shard_map.93), calls=%async_computation.6 | async-start | bytes 40960 | tf_op jit(solution)/shard_map/all_to_all | solution.py:354
Sparse Core Ops, SparseCore 0:
  10.9 49.8 all-gather.2

commit v4 on v3

--- a/solution.py
+++ b/solution.py
@@ -82,28 +82,29 @@
     for copy in copies:
         copy.start()
 
-    def rows_hat(turn, carry):
-        rows = pl.ds(pl.multiple_of(turn * 128, 128), 128)
-        hat_ref[rows, :] = unit_rows(raw[rows, :])[0].astype(BF16)
-        return carry
+    def rows_hat(first, last):
+        for start in range(first, last, 64):
+            rows = slice(start, start + 64)
+            hat_ref[rows] = unit_rows(raw[rows])[0].astype(BF16)
 
     mine = place_ref[2] * 128
     copies[0].wait()
-    lax.fori_loop(ROWS // 128, (ROWS + NEW_DEV) // 128, rows_hat, 0)
+    rows_hat(ROWS, ROWS + NEW_DEV)
     half[:128] = hat_ref[pl.ds(pl.multiple_of(ROWS + mine, 128), 128), :]
     copies[1].wait()
     half[128:] = raw[pl.ds(pl.multiple_of(mine, 128), 128), :]
     half_copy = pltpu.make_async_copy(half, half_hbm, half_sem)
     half_copy.start()
+    rows_hat(0, NEW_DEV)
     copies[2].wait()
-    lax.fori_loop(0, ROWS // 128, rows_hat, 0)
+    rows_hat(NEW_DEV, ROWS)
     half_copy.wait()
 
 
 def scores_body(
-    hat, owner_ref, proto_hbm,
+    hat, owner_hbm, proto_hbm,
     scores_ref, cross_ref, message_ref, partial_ref,
-    raw_proto, product_even, product_odd, total, sums, proto_sems,
+    raw_proto, proto_hat, total, sums, owner, proto_sems, owner_sem,
 ):
     def proto_copy(turn):
         rows = pl.ds(turn * 256, 256)
@@ -113,41 +114,48 @@
     copies = [proto_copy(turn) for turn in range(n_tiles)]
     for copy in copies:
         copy.start()
+    owner_copy = pltpu.make_async_copy(owner_hbm, owner, owner_sem)
+    owner_copy.start()
     total[...] = jnp.zeros_like(total)
     sums[...] = jnp.zeros_like(sums)
-    sums[K_DEV // 128 : K_DEV // 128 + 2] = owner_ref[...].astype(F32)
-    buffers = (product_even, product_odd)
-
-    def multiply(turn):
+    steps = [(start, min(512, ROWS - start)) for start in range(0, ROWS, 512)]
+
+    def normalize(turn):
         copies[turn].wait()
-        proto = unit_rows(raw_proto[turn * 256 : turn * 256 + 256])[0].astype(BF16)
-        buffers[turn % 2][...] = against(hat[...], proto)
+        span = slice(turn * 256, turn * 256 + 256)
+        proto_hat[turn % 2] = unit_rows(raw_proto[span])[0].astype(BF16)
 
     def finish(turn):
-        product = buffers[turn % 2]
         lanes = slice(turn * 256, turn * 256 + 256)
+        proto = proto_hat[turn % 2]
         column = jnp.zeros((8, 256), F32)
-        for start in range(0, ROWS, 64):
+        for first, length in steps:
+            product = against(hat[first : first + length], proto)
+            for start in range(0, length, 64):
+                rows = slice(first + start, first + start + 64)
+                scores = jnp.exp2(product[start : start + 64] * TEACHER_EXP2)
+                scores_ref[rows, lanes] = scores
+                column += jnp.sum(scores.reshape(8, 8, 256), axis=0)
+        product = against(hat[ROWS:], proto)
+        for start in range(0, NEW_DEV, 64):
             rows = slice(start, start + 64)
-            scores = jnp.exp2(product[rows] * TEACHER_EXP2)
-            scores_ref[rows, lanes] = scores
-            column += jnp.sum(scores.reshape(8, 8, 256), axis=0)
-            if start < NEW_DEV:
-                logits = product[ROWS + start : ROWS + start + 64]
-                cross_ref[rows, lanes] = scores * (logits * (1.0 / student_temp))
-                exped = jnp.exp2(logits * STUDENT_EXP2)
-                total[rows] += exped[:, :128] + exped[:, 128:]
+            logits = product[rows]
+            cross_ref[rows, lanes] = scores_ref[rows, lanes] * (logits * (1.0 / student_temp))
+            exped = jnp.exp2(logits * STUDENT_EXP2)
+            total[rows] += exped[:, :128] + exped[:, 128:]
         column = jnp.sum(column, axis=0, keepdims=True)
         sums[2 * turn : 2 * turn + 1] = column[:, :128]
         sums[2 * turn + 1 : 2 * turn + 2] = column[:, 128:]
 
-    multiply(0)
+    normalize(0)
     for turn in range(n_tiles):
         if turn + 1 < n_tiles:
-            multiply(turn + 1)
+            normalize(turn + 1)
         finish(turn)
     for part in range(NEW_DEV // 128):
         partial_ref[part : part + 1] = lane_sums(total[part * 128 : part * 128 + 128])
+    owner_copy.wait()
+    sums[K_DEV // 128 : K_DEV // 128 + 2] = owner[...].astype(F32)
     message = sums[...].astype(BF16)
     for peer in range(message_ref.shape[0]):
         message_ref[peer] = message
@@ -327,7 +335,6 @@
         student_copies[part].start()
     loss_at = 2 * NEW_DEV
     loss_ref[...] = jnp.sum(got_ref[:, :, loss_at : loss_at + 1], axis=0) * (1.0 / n_new)
-    unit_gradient = None
     for part in range(n_parts):
         soft_copies[part].wait()
         for chunk in range(part * step, part * step + step):
@@ -337,14 +344,10 @@
             value = soft[:, lanes] * (factor / got_ref[plane, :, others])
             target = scores_ref[:, lanes] * got_ref[plane, :, names]
             gradient[:, lanes] = (value - target).astype(BF16)
-        student_copies[part].wait()
-        students = student[part * step : part * step + step].reshape(step * 128, FEATURE_WIDTH)
-        piece = jnp.dot(
-            gradient[:, part * step * 128 : (part + 1) * step * 128],
-            students,
-            preferred_element_type=F32,
-        )
-        unit_gradient = piece if part == 0 else unit_gradient + piece
+    for copy in student_copies:
+        copy.wait()
+    students = student[...].reshape(n_new, FEATURE_WIDTH)
+    unit_gradient = jnp.dot(gradient[...], students, preferred_element_type=F32)
     unit = unit_ref[...]
     along = jnp.sum(unit * unit_gradient, axis=1, keepdims=True)
     out_ref[...] = (unit_gradient - unit * along) / length_ref[...]
@@ -399,18 +402,19 @@
             shape((n_sample, K_DEV // 128 + 8, 128), BF16),
             shape((NEW_DEV // 128, 128)),
         ),
-        (hat, owners.reshape(NEW_DEV // 128, 128), in_hbm(prototypes)),
+        (hat, in_hbm(owners.reshape(NEW_DEV // 128, 128)), in_hbm(prototypes)),
         10,
         2 * (ROWS + NEW_DEV) * K_DEV * FEATURE_WIDTH,
         [
             pltpu.VMEM((K_DEV, FEATURE_WIDTH), BF16),
-            pltpu.VMEM((ROWS + NEW_DEV, 256), F32),
-            pltpu.VMEM((ROWS + NEW_DEV, 256), F32),
+            pltpu.VMEM((2, 256, FEATURE_WIDTH), BF16),
             pltpu.VMEM((NEW_DEV, 128), F32),
             pltpu.VMEM((K_DEV // 128 + 8, 128), F32),
+            pltpu.VMEM((NEW_DEV // 128, 128), jnp.int32),
             DMA((K_DEV // 256,)),
+            DMA,
         ],
-        in_specs=[VMEM, VMEM, HBM],
+        in_specs=[VMEM, HBM, HBM],
     )
     first = got = exchange(message, "sample")
     for iteration in range(ITERS - 1):

time: 142 us -> 137 us (0.965)
  Pallas kernels: 29.5 us -> 25.6 us
    pallas_call x10, Pallas kernels: 29.5 us -> 25.6 us  [call(): pl.pallas_call(body, out_shape=out_shape, in_specs=in_specs or [VMEM] * l...]
  transfers between devices with their start and end apart: 2 -> 2, of which waited for: 0 -> 0; matrix products, arithmetic and copies ran while one was open for 0% -> 0% of each run, Pallas kernels for 16% -> 14%
where the time goes in v4:
time: 137 us
  blocking collectives  92.8 us (68%)
  Pallas kernels  25.6 us (19%)
  between operations  14.8 us (11%)
  starting transfers between devices  3.55 us (3%)
    all_to_all x6, blocking collectives, exchange(): lax.all_to_all(message, axis, split_axis=0, concat_axis=0, tiled=True)  92.8 us
    pallas_call x10, Pallas kernels, call(): pl.pallas_call(body, out_shape=out_shape, in_specs=in_specs or [VMEM] * l...  25.6 us
    all_to_all x1, starting transfers between devices, exchange(): lax.all_to_all(message, axis, split_axis=0, concat_axis=0, tiled=True)  3.52 us
  transfers between devices with their start and end apart: 2, of which 0 were waited for; matrix products, arithmetic and copies ran while one was open for 0% of the time, Pallas kernels for 14%

profile of v4, /device:TPU:1, one launch (start us, length us, event | category | flops | bytes accessed | tf_op | source)
XLA Modules:
  0.0 136.8 jit_solution(6067489098354741197)
XLA Ops:
  7.2 0.0 all-gather.3.cloned.1.call-start
  7.9 0.1 pad_add_fusion.place_ref
  7.9 2.4 %shard_map.85 = (bf16[1280,384]{1,0:T(8,128)(2,1)S(1)}, bf16[256,384]{1,0:T(8,128)(2,1)}) custom-call(s32[3]{0:T(128)S(1)} %pad_add_fusion.place_ref, bf16[256,384]{1,0:T(8,128)(2,1)} %new_hbm.1, bf16[768,384]{1,0:T(8,128)(2,1)} %queue_hbm.3, bf16[256,384]{1,0:T(8,128)(2,1)} %student_hbm.1), custom_call_target="tpu_custom_call" | custom-call | flops 3932160 | tf_op jit(solution)/shard_map/pallas_call | solution.py:37
  10.4 0.0 all-gather.3.cloned.1.call-update
  10.4 6.0 %shard_map.86 = (f32[1024,2048]{1,0:T(8,128)S(1)}, f32[256,2048]{1,0:T(8,128)S(1)}, bf16[8,24,128]{2,1,0:T(8,128)(2,1)S(1)}, f32[2,128]{1,0:T(2,128)S(1)}) custom-call(bf16[1280,384]{1,0:T(8,128)(2,1)S(1)} %get-tuple-element.18.hat, s32[2,128]{1,0:T(2,128)} %bitcast.7, bf16[2048,384]{1,0:T(8,128)(2,1)} %proto_hbm.3), custom_call_target="tpu_custom_call" | custom-call | flops 2013265920 | tf_op jit(solution)/shard_map/pallas_call | solution.py:37
  16.4 17.7 %all_to_all.35.got_ref.first_ref = bf16[8,24,128]{2,1,0:T(8,128)(2,1)S(1)} all-to-all(bf16[8,24,128]{2,1,0:T(8,128)(2,1)S(1)} %get-tuple-element.19), channel_id=1, replica_groups=mesh['proto_0'=8,'proto_1'=4,'proto_2'=2,'sample'=8] {'sample'}, dimensions={0} | all-to-all | bytes 98304 | tf_op jit(solution)/shard_map/all_to_all | solution.py:357
  34.1 0.7 shard_map.87
  34.8 23.2 %all_to_all.36.got_ref = bf16[64,8,128]{2,1,0:T(8,128)(2,1)S(1)} all-to-all(bf16[64,8,128]{2,1,0:T(8,128)(2,1)S(1)} %shard_map.87), channel_id=1, replica_groups=mesh['proto_0'=8,'proto_1'=4,'proto_2'=2,'sample'=8] {'proto_0','proto_1..., dimensions={0} | all-to-all | bytes 262144 | tf_op jit(solution)/shard_map/all_to_all | solution.py:357
  58.0 0.8 shard_map.88
  58.8 9.2 %all_to_all.37.got_ref = bf16[8,16,128]{2,1,0:T(8,128)(2,1)S(1)} all-to-all(bf16[8,16,128]{2,1,0:T(8,128)(2,1)S(1)} %shard_map.88), channel_id=1, replica_groups=mesh['proto_0'=8,'proto_1'=4,'proto_2'=2,'sample'=8] {'sample'}, dimensions={0} | all-to-all | bytes 65536 | tf_op jit(solution)/shard_map/all_to_all | solution.py:357
  68.1 0.7 shard_map.89
  68.8 16.0 %all_to_all.38.got_ref = bf16[64,8,128]{2,1,0:T(8,128)(2,1)S(1)} all-to-all(bf16[64,8,128]{2,1,0:T(8,128)(2,1)S(1)} %shard_map.89), channel_id=1, replica_groups=mesh['proto_0'=8,'proto_1'=4,'proto_2'=2,'sample'=8] {'proto_0','proto_1..., dimensions={0} | all-to-all | bytes 262144 | tf_op jit(solution)/shard_map/all_to_all | solution.py:357
  84.8 0.8 shard_map.90
  85.6 9.5 %all_to_all.39.got_ref = f32[8,16,128]{2,1,0:T(8,128)S(1)} all-to-all(f32[8,16,128]{2,1,0:T(8,128)S(1)} %shard_map.90), channel_id=1, replica_groups=mesh['proto_0'=8,'proto_1'=4,'proto_2'=2,'sample'=8] {'sample'}, dimensions={0} | all-to-all | bytes 131072 | tf_op jit(solution)/shard_map/all_to_all | solution.py:357
  95.1 0.4 shard_map.91
  95.5 17.0 %all_to_all.40.got_ref = f32[64,1,768]{2,1,0:T(1,128)S(1)} all-to-all(f32[64,1,768]{2,1,0:T(1,128)S(1)} %get-tuple-element.26), channel_id=1, replica_groups=mesh['proto_0'=8,'proto_1'=4,'proto_2'=2,'sample'=8] {'proto_0','proto_1..., dimensions={0} | all-to-all | bytes 393216 | tf_op jit(solution)/shard_map/all_to_all | solution.py:357
  112.5 0.8 shard_map.93
  113.3 3.5 %all-to-all-start.6 = ((f32[8,1,640]{2,1,0:T(1,128)}), f32[8,1,640]{2,1,0:T(1,128)S(1)}, u32[]{:S(2)}, u32[]{:S(2)}) async-start(f32[8,1,640]{2,1,0:T(1,128)} %shard_map.93), calls=%async_computation.6 | async-start | bytes 40960 | tf_op jit(solution)/shard_map/all_to_all | solution.py:357
  116.8 0.0 all-gather.3.cloned.1.call-done
  116.9 9.4 %shard_map.92 = (f32[256,2048]{1,0:T(8,128)S(1)}, f32[256,2048]{1,0:T(8,128)}, f32[256,384]{1,0:T(8,128)S(1)}, f32[256,1]{1,0:T(8,128)S(1)}, bf16[768,384]{1,0:T(8,128)(2,1)}) custom-call(s32[3]{0:T(128)S(1)} %pad_add_fusion.place_ref, bf16[8,24,128]{2,1,0:T(8,128)(2,1)S(1)} %all_to_all.35.got_ref.first_ref, bf16[16,256,384]{2,1,0:T(8,128)(2,1)} %bitcast.5, ...), custom_call_target="tpu_custom_call" | custom-call | flops 805306368 | tf_op jit(solution)/shard_map/pallas_call | solution.py:37
  126.3 0.0 all-to-all-done.6.got_ref
  126.3 3.6 %shard_map.94 = (f32[256,384]{1,0:T(8,128)}, f32[1,1]{1,0:T(1,128)}) custom-call(f32[8,1,640]{2,1,0:T(1,128)S(1)} %all-to-all-done.6.got_ref, f32[256,2048]{1,0:T(8,128)S(1)} %get-tuple-element.27.scores_ref, f32[256,2048]{1,0:T(8,128)} %get-tuple-element.28.soft_hbm, bf16[16,256,384]{2,1,0:T(8,128)(2,1)} %bitcast.6, ...), custom_call_target="tpu_custom_call" | custom-call | flops 402653184 | tf_op jit(solution)/shard_map/pallas_call | solution.py:37
Async XLA Ops:
  7.2 109.7 %all-gather.3.cloned.1.call-start = ((), (), s32[]{:S(2)}) async-start(), calls=%async_computation.7 | async-start | bytes 3342336 | tf_op jit(solution)/shard_map/all_gather | solution.py:396
  113.3 13.0 %all-to-all-start.6 = ((f32[8,1,640]{2,1,0:T(1,128)}), f32[8,1,640]{2,1,0:T(1,128)S(1)}, u32[]{:S(2)}, u32[]{:S(2)}) async-start(f32[8,1,640]{2,1,0:T(1,128)} %shard_map.93), calls=%async_computation.6 | async-start | bytes 40960 | tf_op jit(solution)/shard_map/all_to_all | solution.py:357
Sparse Core Ops, SparseCore 0:
  10.7 50.0 all-gather.2

commit v5 on v4

--- a/solution.py
+++ b/solution.py
@@ -71,45 +71,22 @@
     return jnp.broadcast_to(row, (128, 128)).T
 
 
-def units_body(
-    place_ref, new_hbm, queue_hbm, student_hbm, hat_ref, half_hbm, raw, half, row_sems, half_sem
-):
-    copies = [
-        pltpu.make_async_copy(student_hbm, raw.at[pl.ds(ROWS, NEW_DEV)], row_sems.at[0]),
-        pltpu.make_async_copy(new_hbm, raw.at[pl.ds(0, NEW_DEV)], row_sems.at[1]),
-        pltpu.make_async_copy(queue_hbm, raw.at[pl.ds(NEW_DEV, QUEUE_PER_INDEX)], row_sems.at[2]),
-    ]
-    for copy in copies:
-        copy.start()
-
-    def rows_hat(first, last):
-        for start in range(first, last, 64):
-            rows = slice(start, start + 64)
-            hat_ref[rows] = unit_rows(raw[rows])[0].astype(BF16)
-
-    mine = place_ref[2] * 128
-    copies[0].wait()
-    rows_hat(ROWS, ROWS + NEW_DEV)
-    half[:128] = hat_ref[pl.ds(pl.multiple_of(ROWS + mine, 128), 128), :]
-    copies[1].wait()
-    half[128:] = raw[pl.ds(pl.multiple_of(mine, 128), 128), :]
-    half_copy = pltpu.make_async_copy(half, half_hbm, half_sem)
-    half_copy.start()
-    rows_hat(0, NEW_DEV)
-    copies[2].wait()
-    rows_hat(NEW_DEV, ROWS)
-    half_copy.wait()
-
-
 def scores_body(
-    hat, owner_hbm, proto_hbm,
+    new_hbm, queue_hbm, student_hbm, owner_hbm, proto_hbm,
     scores_ref, cross_ref, message_ref, partial_ref,
-    raw_proto, proto_hat, total, sums, owner, proto_sems, owner_sem,
+    raw, hat, raw_proto, proto_hat, total, sums, owner, row_sems, proto_sems, owner_sem,
 ):
     def proto_copy(turn):
         rows = pl.ds(turn * 256, 256)
         return pltpu.make_async_copy(proto_hbm.at[rows], raw_proto.at[rows], proto_sems.at[turn])
 
+    row_copies = [
+        pltpu.make_async_copy(new_hbm, raw.at[pl.ds(0, NEW_DEV)], row_sems.at[0]),
+        pltpu.make_async_copy(queue_hbm, raw.at[pl.ds(NEW_DEV, QUEUE_PER_INDEX)], row_sems.at[1]),
+        pltpu.make_async_copy(student_hbm, raw.at[pl.ds(ROWS, NEW_DEV)], row_sems.at[2]),
+    ]
+    for copy in row_copies:
+        copy.start()
     n_tiles = K_DEV // 256
     copies = [proto_copy(turn) for turn in range(n_tiles)]
     for copy in copies:
@@ -121,7 +98,6 @@
     steps = [(start, min(512, ROWS - start)) for start in range(0, ROWS, 512)]
 
     def normalize(turn):
-        copies[turn].wait()
         span = slice(turn * 256, turn * 256 + 256)
         proto_hat[turn % 2] = unit_rows(raw_proto[span])[0].astype(BF16)
 
@@ -147,7 +123,15 @@
         sums[2 * turn : 2 * turn + 1] = column[:, :128]
         sums[2 * turn + 1 : 2 * turn + 2] = column[:, 128:]
 
+    for copy in row_copies:
+        copy.wait()
+    copies[0].wait()
+    for start in range(0, ROWS + NEW_DEV, 64):
+        rows = slice(start, start + 64)
+        hat[rows] = unit_rows(raw[rows])[0].astype(BF16)
     normalize(0)
+    for copy in copies[1:]:
+        copy.wait()
     for turn in range(n_tiles):
         if turn + 1 < n_tiles:
             normalize(turn + 1)
@@ -222,29 +206,32 @@
 
 
 def gathered_body(
-    factor, place_ref, first_ref, everyone_hbm, queue_hbm, proto_hbm, scale_ref,
-    scores_ref, soft_hbm, unit_ref, length_ref, out_ref,
-    rows_in, proto_in, queue_in, soft, chosen, row_sems, soft_sems, proto_sem, queue_sem,
+    factor, place_ref, first_ref, student_hbm, teacher_hbm, queue_hbm, proto_hbm, scale_ref,
+    scores_ref, soft_hbm, hat_hbm, unit_ref, length_ref, out_ref,
+    students, teachers, proto_in, queue_in, soft, hat, chosen,
+    in_sems, soft_sems, hat_sems, proto_sem, queue_sem,
 ):
-    n_blocks = everyone_hbm.shape[0]
-    n_new = n_blocks * 128
+    n_new = student_hbm.shape[0]
     share = unit_ref.shape[0]
     first = pl.multiple_of(place_ref[0] * share, share)
+    n_parts = soft_sems.shape[0]
+    step = n_new // n_parts
+    student_copy = pltpu.make_async_copy(student_hbm, students, in_sems.at[0])
+    teacher_copy = pltpu.make_async_copy(teacher_hbm, teachers, in_sems.at[1])
     proto_copy = pltpu.make_async_copy(proto_hbm.at[pl.ds(first, share)], proto_in, proto_sem)
+    queue_copy = pltpu.make_async_copy(queue_hbm, queue_in, queue_sem)
     proto_copy.start()
-
-    def rows_copy(turn):
-        blocks = pl.ds(turn * 2, 2)
-        return pltpu.make_async_copy(everyone_hbm.at[blocks], rows_in.at[blocks], row_sems.at[turn])
-
-    def soft_copy(turn):
-        lanes = pl.ds(pl.multiple_of(turn * 256, 256), 256)
-        return pltpu.make_async_copy(soft.at[:, lanes], soft_hbm.at[:, lanes], soft_sems.at[turn])
-
-    for turn in range(n_blocks // 2):
-        rows_copy(turn).start()
-    queue_copy = pltpu.make_async_copy(queue_hbm, queue_in, queue_sem)
+    student_copy.start()
+    teacher_copy.start()
     queue_copy.start()
+
+    def out_copies(part):
+        span = pl.ds(part * step, step)
+        return (
+            pltpu.make_async_copy(soft.at[:, span], soft_hbm.at[:, span], soft_sems.at[part]),
+            pltpu.make_async_copy(hat.at[span], hat_hbm.at[span], hat_sems.at[part]),
+        )
+
     columns = [
         along_rows(scale_ref[pl.ds(place_ref[0] * 2 + part, 1), :] * factor)
         for part in range(share // 128)
@@ -254,23 +241,22 @@
     unit_ref[...] = unit
     length_ref[...] = length
     proto = unit.astype(BF16)
-
-    def tile(turn, carry):
-        start = pl.multiple_of(turn * 256, 256)
-        rows_copy(turn).wait()
-        for side in range(2):
-            lanes = pl.ds(pl.multiple_of(start + side * 128, 128), 128)
-            exped = jnp.exp2(against(proto, rows_in[turn * 2 + side, :128, :]) * STUDENT_EXP2)
-            soft[:, lanes] = exped
-            teacher = unit_rows(rows_in[turn * 2 + side, 128:, :])[0].astype(BF16)
-            scores = jnp.exp2(against(proto, teacher) * TEACHER_EXP2)
-            for part in range(2):
-                block = slice(part * 128, part * 128 + 128)
-                scores_ref[block, lanes] = scores[block] * columns[part]
-        soft_copy(turn).start()
-        return carry
-
-    lax.fori_loop(0, n_blocks // 2, tile, 0)
+    student_copy.wait()
+    for part in range(n_parts):
+        for start in range(part * step, part * step + step, 128):
+            rows = slice(start, start + 128)
+            hat[rows] = unit_rows(students[rows])[0].astype(BF16)
+            soft[:, rows] = jnp.exp2(against(proto, hat[rows]) * STUDENT_EXP2)
+        for copy in out_copies(part):
+            copy.start()
+    teacher_copy.wait()
+    for start in range(0, n_new, 128):
+        rows = slice(start, start + 128)
+        teacher = unit_rows(teachers[rows])[0].astype(BF16)
+        scores = jnp.exp2(against(proto, teacher) * TEACHER_EXP2)
+        for part in range(2):
+            block = slice(part * 128, part * 128 + 128)
+            scores_ref[block, rows] = scores[block] * columns[part]
 
     mine = place_ref[0].astype(F32)
     head = place_ref[1].astype(F32)
@@ -291,14 +277,14 @@
         slot = jnp.where(named > 0.5, slot, -1.0)
         chosen[:, chunk * 128 : chunk * 128 + 128] = jnp.where(slots == slot, 1.0, 0.0).astype(BF16)
         base += jnp.sum(named, axis=1, keepdims=True)
-    teachers = rows_in[:, 128:, :].reshape(n_new, FEATURE_WIDTH)
-    got = jnp.dot(chosen[...], teachers, preferred_element_type=F32)
+    got = jnp.dot(chosen[...], teachers[...], preferred_element_type=F32)
     turn = lax.broadcasted_iota(jnp.int32, (QUEUE_PER_INDEX, FEATURE_WIDTH), 0).astype(F32) - head
     turn = jnp.where(turn < 0.0, turn + size, turn)
     queue_copy.wait()
     out_ref[...] = jnp.where(turn < base, got, queue_in[...].astype(F32)).astype(BF16)
-    for turn in range(n_blocks // 2):
-        soft_copy(turn).wait()
+    for part in range(n_parts):
+        for copy in out_copies(part):
+            copy.wait()
 
 
 def rows_body(got_ref, out_ref):
@@ -312,24 +298,20 @@
 
 
 def gradient_body(
-    factor, got_ref, scores_ref, soft_hbm, everyone_hbm, unit_ref, length_ref, out_ref, loss_ref,
+    factor, got_ref, scores_ref, soft_hbm, student_hbm, unit_ref, length_ref, out_ref, loss_ref,
     soft, student, gradient, soft_sems, student_sems,
 ):
-    n_blocks = student.shape[0]
-    n_new = n_blocks * 128
+    n_new = student.shape[0]
     n_parts = soft_sems.shape[0]
-    step = n_blocks // n_parts
+    step = n_new // 128 // n_parts
     soft_copies, student_copies = [], []
     for part in range(n_parts):
-        lanes = pl.ds(part * step * 128, step * 128)
+        span = pl.ds(part * step * 128, step * 128)
         soft_copies.append(
-            pltpu.make_async_copy(soft_hbm.at[:, lanes], soft.at[:, lanes], soft_sems.at[part])
+            pltpu.make_async_copy(soft_hbm.at[:, span], soft.at[:, span], soft_sems.at[part])
         )
-        blocks = pl.ds(part * step, step)
         student_copies.append(
-            pltpu.make_async_copy(
-                everyone_hbm.at[blocks, pl.ds(0, 128), :], student.at[blocks], student_sems.at[part]
-            )
+            pltpu.make_async_copy(student_hbm.at[span], student.at[span], student_sems.at[part])
         )
         soft_copies[part].start()
         student_copies[part].start()
@@ -346,8 +328,7 @@
             gradient[:, lanes] = (value - target).astype(BF16)
     for copy in student_copies:
         copy.wait()
-    students = student[...].reshape(n_new, FEATURE_WIDTH)
-    unit_gradient = jnp.dot(gradient[...], students, preferred_element_type=F32)
+    unit_gradient = jnp.dot(gradient[...], student[...], preferred_element_type=F32)
     unit = unit_ref[...]
     along = jnp.sum(unit * unit_gradient, axis=1, keepdims=True)
     out_ref[...] = (unit_gradient - unit * along) / length_ref[...]
@@ -371,29 +352,11 @@
         [
             my_index.astype(jnp.int32),
             queue_oldest_slot[0].astype(jnp.int32),
-            lax.axis_index("proto_2").astype(jnp.int32),
         ]
     )
 
-    hat, half = call(
-        units_body,
-        (
-            shape((ROWS + NEW_DEV, FEATURE_WIDTH), BF16),
-            pltpu.HBM((NEW_DEV, FEATURE_WIDTH), BF16),
-        ),
-        (place, in_hbm(teacher_new), in_hbm(queue), in_hbm(student)),
-        6,
-        8 * (ROWS + NEW_DEV) * FEATURE_WIDTH,
-        [
-            pltpu.VMEM((ROWS + NEW_DEV, FEATURE_WIDTH), BF16),
-            pltpu.VMEM((NEW_DEV, FEATURE_WIDTH), BF16),
-            DMA((3,)),
-            DMA,
-        ],
-        in_specs=[SMEM] + [HBM] * 3,
-        out_specs=(VMEM, HBM),
-    )
-    everyone = lax.all_gather(half, ("sample", "proto_2"), axis=0)
+    all_students = lax.all_gather(student, "sample", axis=0, tiled=True)
+    all_teachers = lax.all_gather(teacher_new, "sample", axis=0, tiled=True)
     scores, cross, message, partial = call(
         scores_body,
         (
@@ -402,19 +365,28 @@
             shape((n_sample, K_DEV // 128 + 8, 128), BF16),
             shape((NEW_DEV // 128, 128)),
         ),
-        (hat, in_hbm(owners.reshape(NEW_DEV // 128, 128)), in_hbm(prototypes)),
+        (
+            in_hbm(teacher_new),
+            in_hbm(queue),
+            in_hbm(student),
+            in_hbm(owners.reshape(NEW_DEV // 128, 128)),
+            in_hbm(prototypes),
+        ),
         10,
         2 * (ROWS + NEW_DEV) * K_DEV * FEATURE_WIDTH,
         [
+            pltpu.VMEM((ROWS + NEW_DEV, FEATURE_WIDTH), BF16),
+            pltpu.VMEM((ROWS + NEW_DEV, FEATURE_WIDTH), BF16),
             pltpu.VMEM((K_DEV, FEATURE_WIDTH), BF16),
             pltpu.VMEM((2, 256, FEATURE_WIDTH), BF16),
             pltpu.VMEM((NEW_DEV, 128), F32),
             pltpu.VMEM((K_DEV // 128 + 8, 128), F32),
             pltpu.VMEM((NEW_DEV // 128, 128), jnp.int32),
+            DMA((3,)),
             DMA((K_DEV // 256,)),
             DMA,
         ],
-        in_specs=[VMEM, HBM, HBM],
+        in_specs=[HBM] * 5,
     )
     first = got = exchange(message, "sample")
     for iteration in range(ITERS - 1):
@@ -451,41 +423,53 @@
     )
     got = exchange(message, "sample")
 
-    all_scores, all_soft, my_unit, my_length, new_queue = call(
+    all_scores, all_soft, all_hats, my_unit, my_length, new_queue = call(
         functools.partial(gathered_body, factor),
         (
             shape((share, new_total)),
             pltpu.HBM((share, new_total), F32),
+            pltpu.HBM((new_total, FEATURE_WIDTH), BF16),
             shape((share, FEATURE_WIDTH)),
             shape((share, 1)),
             shape((QUEUE_PER_INDEX, FEATURE_WIDTH), BF16),
         ),
-        (place, first, in_hbm(everyone), in_hbm(queue), in_hbm(prototypes), proto_scale),
+        (
+            place,
+            first,
+            in_hbm(all_students),
+            in_hbm(all_teachers),
+            in_hbm(queue),
+            in_hbm(prototypes),
+            proto_scale,
+        ),
         16,
         4 * share * new_total * FEATURE_WIDTH,
         [
-            pltpu.VMEM(everyone.shape, BF16),
+            pltpu.VMEM((new_total, FEATURE_WIDTH), BF16),
+            pltpu.VMEM((new_total, FEATURE_WIDTH), BF16),
             pltpu.VMEM((share, FEATURE_WIDTH), BF16),
             pltpu.VMEM((QUEUE_PER_INDEX, FEATURE_WIDTH), BF16),
             pltpu.VMEM((share, new_total), F32),
+            pltpu.VMEM((new_total, FEATURE_WIDTH), BF16),
             pltpu.VMEM((QUEUE_PER_INDEX, new_total), BF16),
-            DMA((n_sample,)),
-            DMA((n_sample,)),
+            DMA((2,)),
+            DMA((4,)),
+            DMA((4,)),
             DMA,
             DMA,
         ],
-        in_specs=[SMEM, VMEM, HBM, HBM, HBM, VMEM],
-        out_specs=(VMEM, HBM, VMEM, VMEM, VMEM),
+        in_specs=[SMEM, VMEM, HBM, HBM, HBM, HBM, VMEM],
+        out_specs=(VMEM, HBM, HBM, VMEM, VMEM, VMEM),
     )
     proto_grad, loss = call(
         functools.partial(gradient_body, factor),
         (shape((share, FEATURE_WIDTH)), shape((1, 1))),
-        (got, all_scores, in_hbm(all_soft), in_hbm(everyone), my_unit, my_length),
+        (got, all_scores, in_hbm(all_soft), in_hbm(all_hats), my_unit, my_length),
         12,
         2 * share * new_total * FEATURE_WIDTH,
         [
             pltpu.VMEM((share, new_total), F32),
-            pltpu.VMEM((new_total // 128, 128, FEATURE_WIDTH), BF16),
+            pltpu.VMEM((new_total, FEATURE_WIDTH), BF16),
             pltpu.VMEM((share, new_total), BF16),
             DMA((4,)),
             DMA((4,)),

time: 137 us -> 136 us (level)
  blocking collectives: 92.8 us -> 76.6 us
  waiting for transfers between devices: 0.04 us -> 12.9 us
  starting transfers between devices: 3.55 us -> 8.73 us
  Pallas kernels: 25.6 us -> 22.8 us
    all_to_all x6 -> x5, blocking collectives: 92.8 us -> 76.6 us  [exchange(): lax.all_to_all(message, axis, split_axis=0, concat_axis=0, tiled=True)]
    all_to_all x1 -> x2, waiting for transfers between devices: 0.01 us -> 11.5 us  [exchange(): lax.all_to_all(message, axis, split_axis=0, concat_axis=0, tiled=True)]
    all_to_all x1 -> x2, starting transfers between devices: 3.52 us -> 8.66 us  [exchange(): lax.all_to_all(message, axis, split_axis=0, concat_axis=0, tiled=True)]
    pallas_call x10 -> x9, Pallas kernels: 25.6 us -> 22.8 us  [call(): pl.pallas_call(body, out_shape=out_shape, in_specs=in_specs or [VMEM] * l...]
  transfers between devices with their start and end apart: 2 -> 4, of which waited for: 0 -> 1; matrix products, arithmetic and copies ran while one was open for 0% -> 0% of each run, Pallas kernels for 14% -> 14%
where the time goes in v5:
time: 136 us
  blocking collectives  76.6 us (56%)
  Pallas kernels  22.8 us (17%)
  between operations  14.8 us (11%)
  waiting for transfers between devices  12.9 us (9%)
  starting transfers between devices  8.73 us (6%)
    all_to_all x5, blocking collectives, exchange(): lax.all_to_all(message, axis, split_axis=0, concat_axis=0, tiled=True)  76.6 us
    pallas_call x9, Pallas kernels, call(): pl.pallas_call(body, out_shape=out_shape, in_specs=in_specs or [VMEM] * l...  22.8 us
    all_to_all x2, waiting for transfers between devices, exchange(): lax.all_to_all(message, axis, split_axis=0, concat_axis=0, tiled=True)  11.5 us
    all_to_all x2, starting transfers between devices, exchange(): lax.all_to_all(message, axis, split_axis=0, concat_axis=0, tiled=True)  8.66 us
  transfers between devices with their start and end apart: 4, of which 1 were waited for; matrix products, arithmetic and copies ran while one was open for 0% of the time, Pallas kernels for 14%

profile of v5, /device:TPU:1, one launch (start us, length us, event | category | flops | bytes accessed | tf_op | source)
XLA Modules:
  0.0 135.9 jit_solution(4264445299874084749)
XLA Ops:
  7.2 0.0 all-gather.3.cloned.1.call-start
  7.2 0.7 all-gather.3.cloned.1.call-update
  7.9 0.0 all-gather.5.cloned.1.call-start
  7.9 0.7 all-gather.5.cloned.1.call-update
  8.6 5.6 %shard_map.85 = (f32[1024,2048]{1,0:T(8,128)S(1)}, f32[256,2048]{1,0:T(8,128)S(1)}, bf16[8,24,128]{2,1,0:T(8,128)(2,1)S(1)}, f32[2,128]{1,0:T(2,128)S(1)}) custom-call(bf16[256,384]{1,0:T(8,128)(2,1)} %new_hbm.1, bf16[768,384]{1,0:T(8,128)(2,1)} %queue_hbm.3, bf16[256,384]{1,0:T(8,128)(2,1)} %student_hbm.1, s32[2,128]{1,0:T(2,128)} %bitcast.3, ...), custom_call_target="tpu_custom_call" | custom-call | flops 2013265920 | tf_op jit(solution)/shard_map/pallas_call | solution.py:37
  14.3 17.7 %all_to_all.35.got_ref.first_ref = bf16[8,24,128]{2,1,0:T(8,128)(2,1)S(1)} all-to-all(bf16[8,24,128]{2,1,0:T(8,128)(2,1)S(1)} %get-tuple-element.17), channel_id=1, replica_groups=mesh['proto_0'=8,'proto_1'=4,'proto_2'=2,'sample'=8] {'sample'}, dimensions={0} | all-to-all | bytes 98304 | tf_op jit(solution)/shard_map/all_to_all | solution.py:338
  32.0 0.7 shard_map.86
  32.7 23.1 %all_to_all.36.got_ref = bf16[64,8,128]{2,1,0:T(8,128)(2,1)S(1)} all-to-all(bf16[64,8,128]{2,1,0:T(8,128)(2,1)S(1)} %shard_map.86), channel_id=1, replica_groups=mesh['proto_0'=8,'proto_1'=4,'proto_2'=2,'sample'=8] {'proto_0','proto_1..., dimensions={0} | all-to-all | bytes 262144 | tf_op jit(solution)/shard_map/all_to_all | solution.py:338
  55.8 0.8 shard_map.87
  56.6 9.2 %all_to_all.37.got_ref = bf16[8,16,128]{2,1,0:T(8,128)(2,1)S(1)} all-to-all(bf16[8,16,128]{2,1,0:T(8,128)(2,1)S(1)} %shard_map.87), channel_id=1, replica_groups=mesh['proto_0'=8,'proto_1'=4,'proto_2'=2,'sample'=8] {'sample'}, dimensions={0} | all-to-all | bytes 65536 | tf_op jit(solution)/shard_map/all_to_all | solution.py:338
  65.8 0.7 shard_map.88
  66.5 16.0 %all_to_all.38.got_ref = bf16[64,8,128]{2,1,0:T(8,128)(2,1)S(1)} all-to-all(bf16[64,8,128]{2,1,0:T(8,128)(2,1)S(1)} %shard_map.88), channel_id=1, replica_groups=mesh['proto_0'=8,'proto_1'=4,'proto_2'=2,'sample'=8] {'proto_0','proto_1..., dimensions={0} | all-to-all | bytes 262144 | tf_op jit(solution)/shard_map/all_to_all | solution.py:338
  82.6 0.8 shard_map.89
  83.3 10.5 %all_to_all.39.got_ref = f32[8,16,128]{2,1,0:T(8,128)S(1)} all-to-all(f32[8,16,128]{2,1,0:T(8,128)S(1)} %shard_map.89), channel_id=1, replica_groups=mesh['proto_0'=8,'proto_1'=4,'proto_2'=2,'sample'=8] {'sample'}, dimensions={0} | all-to-all | bytes 131072 | tf_op jit(solution)/shard_map/all_to_all | solution.py:338
  93.8 1.1 shard_map.90
  94.9 5.1 %all-to-all-start.5 = ((f32[64,1,768]{2,1,0:T(1,128)}), f32[64,1,768]{2,1,0:T(1,128)S(1)}, u32[]{:S(2)}, u32[]{:S(2)}) async-start(f32[64,1,768]{2,1,0:T(1,128)} %get-tuple-element.23), calls=%async_computation.5 | async-start | bytes 393216 | tf_op jit(solution)/shard_map/all_to_all | solution.py:338
  100.7 0.1 pad_add_fusion.place_ref
  100.8 11.5 %all-to-all-done.5.got_ref = f32[64,1,768]{2,1,0:T(1,128)S(1)} async-done(((f32[64,1,768]{2,1,0:T(1,128)}), f32[64,1,768]{2,1,0:T(1,128)S(1)}, u32[]{:S(2)}, u32[]{:S(2)}) %all-to-all-start.5) | async-done | bytes 196640 | tf_op jit(solution)/shard_map/all_to_all | solution.py:338
  112.3 0.8 shard_map.92
  113.1 3.5 %all-to-all-start.6 = ((f32[8,1,640]{2,1,0:T(1,128)}), f32[8,1,640]{2,1,0:T(1,128)S(1)}, u32[]{:S(2)}, u32[]{:S(2)}) async-start(f32[8,1,640]{2,1,0:T(1,128)} %shard_map.92), calls=%async_computation.6 | async-start | bytes 40960 | tf_op jit(solution)/shard_map/all_to_all | solution.py:338
  116.6 0.0 all-gather.3.cloned.1.call-done.student_hbm
  116.6 0.0 all-gather.5.cloned.1.call-done.teacher_hbm
  116.7 8.7 %shard_map.91 = (f32[256,2048]{1,0:T(8,128)S(1)}, f32[256,2048]{1,0:T(8,128)}, bf16[2048,384]{1,0:T(8,128)(2,1)}, f32[256,384]{1,0:T(8,128)S(1)}, f32[256,1]{1,0:T(8,128)S(1)}, /*index=5*/bf16[768,384]{1,0:T(8,128)(2,1)}) custom-call(s32[2]{0:T(128)S(1)} %pad_add_fusion.place_ref, bf16[8,24,128]{2,1,0:T(8,128)(2,1)S(1)} %all_to_all.35.got_ref.first_ref, ...), custom_call_target="tpu_custom_call" | custom-call | flops 805306368 | tf_op jit(solution)/shard_map/pallas_call | solution.py:37
  125.4 0.0 all-to-all-done.6.got_ref
  125.4 3.6 %shard_map.93 = (f32[256,384]{1,0:T(8,128)}, f32[1,1]{1,0:T(1,128)}) custom-call(f32[8,1,640]{2,1,0:T(1,128)S(1)} %all-to-all-done.6.got_ref, f32[256,2048]{1,0:T(8,128)S(1)} %get-tuple-element.24.scores_ref, f32[256,2048]{1,0:T(8,128)} %get-tuple-element.25.soft_hbm, bf16[2048,384]{1,0:T(8,128)(2,1)} %get-tuple-element.26.student_hbm, ...), custom_call_target="tpu_custom_call" | custom-call | flops 402653184 | tf_op jit(solution)/shard_map/pallas_call | solution.py:37
Async XLA Ops:
  7.2 109.5 %all-gather.3.cloned.1.call-start = ((), (), s32[]{:S(2)}) async-start(), calls=%async_computation.7 | async-start | bytes 1769472 | tf_op jit(solution)/shard_map/all_gather | solution.py:358
  7.9 108.8 %all-gather.5.cloned.1.call-start = ((), (), s32[]{:S(2)}) async-start(), calls=%async_computation.8 | async-start | bytes 1769472 | tf_op jit(solution)/shard_map/all_gather | solution.py:359
  94.9 17.4 %all-to-all-start.5 = ((f32[64,1,768]{2,1,0:T(1,128)}), f32[64,1,768]{2,1,0:T(1,128)S(1)}, u32[]{:S(2)}, u32[]{:S(2)}) async-start(f32[64,1,768]{2,1,0:T(1,128)} %get-tuple-element.23), calls=%async_computation.5 | async-start | bytes 393216 | tf_op jit(solution)/shard_map/all_to_all | solution.py:338
  113.1 12.3 %all-to-all-start.6 = ((f32[8,1,640]{2,1,0:T(1,128)}), f32[8,1,640]{2,1,0:T(1,128)S(1)}, u32[]{:S(2)}, u32[]{:S(2)}) async-start(f32[8,1,640]{2,1,0:T(1,128)} %shard_map.92), calls=%async_computation.6 | async-start | bytes 40960 | tf_op jit(solution)/shard_map/all_to_all | solution.py:338
Sparse Core Ops, SparseCore 0:
  10.1 44.4 all-gather.2
  56.7 40.9 all-gather.4
